TPU v7x, 256 devices: a whole 4x4x8 slice. The times are simulated.
256 devices in a mesh: dp: 128 (over x, y_lo, z, core), rep: 2 (over y_hi).
Axes of the slice: x: 4, y: 4 (y_hi: 2, y_lo: 2; y = y_hi * 2 + y_lo), z: 8, core: 2. Of those that a mesh axis runs over, the one named last changes fastest.
Arguments:
- images: bfloat16 [131072, 512], P(('dp', 'rep')), may hold values from -6 to 6
- text_feats: bfloat16 [131072, 768], P(('dp', 'rep')), may hold values from -24 to 24
- text_proj: bfloat16 [768, 512], replicated, may hold values from -0.21875 to 0.21875
- logit_scale: float32 [1], replicated, may hold values from 4 to 16
- logit_bias: float32 [1], replicated, may hold values from -6 to -2
Outputs:
- image_grad: bfloat16 [131072, 512], P(('dp', 'rep'))
- proj_grad: float32 [768, 512], P(('dp', 'rep'))
All inputs are finite; a program needn't handle non-finite values.
Results may differ from a plain program's by a relative error of at most 0.013.
Values may be sent and summed in bfloat16 or wider, within the bound.
No kernel may reach another device: no remote copies, remote signals or barrier semaphores. Data moves between devices by JAX's collectives and lax.ppermute only.
A program may use at most 64 MiB of HBM per device.

v0:
```python
import jax
import jax.numpy as jnp
from jax import lax
from jax.sharding import PartitionSpec as P

SHIFTS = 8


EPS = 1e-06


def passed_along(block, axis, distance):
    devices = range(lax.axis_size(axis))
    route = [((i - distance) % len(devices), i) for i in devices]
    return lax.ppermute(block, axis, route)


def unit_rows(values):
    square = jnp.sum(values * values, axis=-1, keepdims=True)
    factor = lax.rsqrt(square + EPS)
    return (values * factor, factor)


def back_rows(normal, factor, upstream):
    return factor * (upstream - normal * jnp.sum(normal * upstream, axis=-1, keepdims=True))


def pass_text(block):
    return passed_along(block, "dp", 1)


def pass_terms(terms):
    return passed_along(terms.astype(jnp.bfloat16), "dp", 1).astype(terms.dtype)


def on_device(images, text_feats, text_proj, logit_scale, logit_bias):
    image_unit, image_factor = unit_rows(images.astype(jnp.float32))
    u_round = image_unit.astype(jnp.bfloat16)
    text_raw = jnp.dot(text_feats, text_proj, preferred_element_type=jnp.float32)
    text_unit, text_factor = unit_rows(text_raw)
    v_round = text_unit.astype(jnp.bfloat16)
    scaling = logit_scale[0]
    shifted = logit_bias[0]
    count_rows = u_round.shape[0]
    positions = jnp.arange(count_rows, dtype=jnp.int32)
    identity_mask = (positions[:, None] == positions[None, :]).astype(jnp.float32)

    def weigh(left, right, label):
        logits = (
            scaling
            * lax.dot_general(
                left, right, (((1,), (1,)), ((), ())), preferred_element_type=jnp.float32
            )
            + shifted
        )
        return (scaling * -label * jax.nn.sigmoid(-label * logits)).astype(jnp.bfloat16)

    def tile(held, label):
        weighted = weigh(u_round, held, label)
        image_part = jnp.dot(weighted, held, preferred_element_type=jnp.float32)
        text_part = lax.dot_general(
            weighted, u_round, (((0,), (0,)), ((), ())), preferred_element_type=jnp.float32
        )
        return (image_part, text_part)

    image_sum, text_sum = tile(v_round, 2.0 * identity_mask - 1.0)
    held = v_round
    carried = None
    for offset in range(1, SHIFTS + 1):
        held = pass_text(held)
        image_part, text_part = tile(held, -1.0)
        image_sum = image_sum + image_part
        if carried is None:
            carried = text_part
        else:
            carried = pass_terms(carried) + text_part
    text_sum = text_sum + passed_along(carried.astype(jnp.bfloat16), "dp", -SHIFTS).astype(
        carried.dtype
    )
    image_grad = back_rows(image_unit, image_factor, image_sum).astype(jnp.bfloat16)
    text_grad = back_rows(text_unit, text_factor, text_sum).astype(jnp.bfloat16)
    proj_grad = lax.psum_scatter(
        lax.dot_general(
            text_feats, text_grad, (((0,), (0,)), ((), ())), preferred_element_type=jnp.float32
        ),
        ("dp", "rep"),
        scatter_dimension=0,
        tiled=True,
    )
    return (image_grad, proj_grad)


def solution(mesh):
    in_specs = (P(("dp", "rep"), None), P(("dp", "rep"), None), P(), P(), P())
    out_specs = (P(("dp", "rep"), None), P(("dp", "rep"), None))
    return jax.shard_map(
        on_device, mesh=mesh, in_specs=in_specs, out_specs=out_specs, check_vma=False
    )
```

profile of v0, /device:TPU:32, one launch (start us, length us, event | category | flops | bytes accessed | tf_op | source)
XLA Modules:
  0.0 422.8 jit_solution(10424807209609507682)
XLA Ops:
  7.2 1.1 copy-done
  8.3 1.8 multiply_reduce_fusion.1
  12.0 0.7 fusion.58
  13.1 5.9 %collective-permute-done = bf16[512,512]{0,1:T(8,128)(2,1)} collective-permute-done((bf16[512,512]{0,1:T(8,128)(2,1)S(1)}, bf16[512,512]{0,1:T(8,128)(2,1)}, u32[]{:S(2)}, u32[]{:S(2)}) %collective-permute-start) | collective-permute-done | bytes 524320 | tf_op jit(solution)/shard_map/ppermute | solution.py:15
  19.0 1.7 fusion.59
  21.1 2.1 collective-permute-start.8
  23.3 1.5 convolution_add_fusion.7
  24.8 3.0 collective-permute-done.1
  28.5 5.0 %collective-permute-done.8 = bf16[512,512]{0,1:T(8,128)(2,1)S(1)} collective-permute-done((bf16[512,512]{0,1:T(8,128)(2,1)S(1)}, bf16[512,512]{0,1:T(8,128)(2,1)S(1)}, u32[]{:S(2)}, u32[]{:S(2)}) %collective-permute-start.8) | collective-permute-done | bytes 524320 | tf_op jit(solution)/shard_map/ppermute | solution.py:15
  34.5 4.6 %collective-permute-done.2 = bf16[512,512]{0,1:T(8,128)(2,1)S(1)} collective-permute-done((bf16[512,512]{0,1:T(8,128)(2,1)S(1)}, bf16[512,512]{0,1:T(8,128)(2,1)S(1)}, u32[]{:S(2)}, u32[]{:S(2)}) %collective-permute-start.2) | collective-permute-done | bytes 524320 | tf_op jit(solution)/shard_map/ppermute | solution.py:15
  40.1 4.5 %collective-permute-done.9 = bf16[512,512]{0,1:T(8,128)(2,1)S(1)} collective-permute-done((bf16[512,512]{0,1:T(8,128)(2,1)S(1)}, bf16[512,512]{0,1:T(8,128)(2,1)S(1)}, u32[]{:S(2)}, u32[]{:S(2)}) %collective-permute-start.9) | collective-permute-done | bytes 524320 | tf_op jit(solution)/shard_map/ppermute | solution.py:15
  45.4 4.9 %collective-permute-done.3 = bf16[512,512]{0,1:T(8,128)(2,1)S(1)} collective-permute-done((bf16[512,512]{0,1:T(8,128)(2,1)S(1)}, bf16[512,512]{0,1:T(8,128)(2,1)S(1)}, u32[]{:S(2)}, u32[]{:S(2)}) %collective-permute-start.3) | collective-permute-done | bytes 524320 | tf_op jit(solution)/shard_map/ppermute | solution.py:15
  51.4 4.5 %collective-permute-done.10 = bf16[512,512]{0,1:T(8,128)(2,1)S(1)} collective-permute-done((bf16[512,512]{0,1:T(8,128)(2,1)S(1)}, bf16[512,512]{0,1:T(8,128)(2,1)S(1)}, u32[]{:S(2)}, u32[]{:S(2)}) %collective-permute-start.10) | collective-permute-done | bytes 524320 | tf_op jit(solution)/shard_map/ppermute | solution.py:15
  56.6 4.9 %collective-permute-done.4 = bf16[512,512]{0,1:T(8,128)(2,1)S(1)} collective-permute-done((bf16[512,512]{0,1:T(8,128)(2,1)S(1)}, bf16[512,512]{0,1:T(8,128)(2,1)S(1)}, u32[]{:S(2)}, u32[]{:S(2)}) %collective-permute-start.4) | collective-permute-done | bytes 524320 | tf_op jit(solution)/shard_map/ppermute | solution.py:15
  62.6 4.5 %collective-permute-done.11 = bf16[512,512]{0,1:T(8,128)(2,1)S(1)} collective-permute-done((bf16[512,512]{0,1:T(8,128)(2,1)S(1)}, bf16[512,512]{0,1:T(8,128)(2,1)S(1)}, u32[]{:S(2)}, u32[]{:S(2)}) %collective-permute-start.11) | collective-permute-done | bytes 524320 | tf_op jit(solution)/shard_map/ppermute | solution.py:15
  67.4 5.6 %collective-permute-done.5 = bf16[512,512]{0,1:T(8,128)(2,1)S(1)} collective-permute-done((bf16[512,512]{0,1:T(8,128)(2,1)S(1)}, bf16[512,512]{0,1:T(8,128)(2,1)S(1)}, u32[]{:S(2)}, u32[]{:S(2)}) %collective-permute-start.5) | collective-permute-done | bytes 524320 | tf_op jit(solution)/shard_map/ppermute | solution.py:15
  73.0 0.6 fusion.64
  74.0 5.8 %collective-permute-done.12 = bf16[512,512]{0,1:T(8,128)(2,1)S(1)} collective-permute-done((bf16[512,512]{0,1:T(8,128)(2,1)S(1)}, bf16[512,512]{0,1:T(8,128)(2,1)S(1)}, u32[]{:S(2)}, u32[]{:S(2)}) %collective-permute-start.12) | collective-permute-done | bytes 524320 | tf_op jit(solution)/shard_map/ppermute | solution.py:15
  80.1 5.7 %collective-permute-done.6 = bf16[512,512]{0,1:T(8,128)(2,1)S(1)} collective-permute-done((bf16[512,512]{0,1:T(8,128)(2,1)S(1)}, bf16[512,512]{0,1:T(8,128)(2,1)S(1)}, u32[]{:S(2)}, u32[]{:S(2)}) %collective-permute-start.6) | collective-permute-done | bytes 524320 | tf_op jit(solution)/shard_map/ppermute | solution.py:15
  86.6 0.8 copy-done.1
  87.8 5.1 %collective-permute-done.13 = bf16[512,512]{0,1:T(8,128)(2,1)S(1)} collective-permute-done((bf16[512,512]{0,1:T(8,128)(2,1)S(1)}, bf16[512,512]{0,1:T(8,128)(2,1)S(1)}, u32[]{:S(2)}, u32[]{:S(2)}) %collective-permute-start.13) | collective-permute-done | bytes 524320 | tf_op jit(solution)/shard_map/ppermute | solution.py:15
  93.1 5.5 %collective-permute-done.7 = bf16[512,512]{0,1:T(8,128)(2,1)S(1)} collective-permute-done((bf16[512,512]{0,1:T(8,128)(2,1)S(1)}, bf16[512,512]{0,1:T(8,128)(2,1)S(1)}, u32[]{:S(2)}, u32[]{:S(2)}) %collective-permute-start.7) | collective-permute-done | bytes 524320 | tf_op jit(solution)/shard_map/ppermute | solution.py:15
  99.4 0.8 copy-done.3
  100.6 5.3 %collective-permute-done.14 = bf16[512,512]{0,1:T(8,128)(2,1)S(1)} collective-permute-done((bf16[512,512]{0,1:T(8,128)(2,1)S(1)}, bf16[512,512]{0,1:T(8,128)(2,1)S(1)}, u32[]{:S(2)}, u32[]{:S(2)}) %collective-permute-start.14) | collective-permute-done | bytes 524320 | tf_op jit(solution)/shard_map/ppermute | solution.py:15
  106.1 4.7 %collective-permute-start.15 = (bf16[512,512]{0,1:T(8,128)(2,1)S(1)}, bf16[512,512]{0,1:T(8,128)(2,1)S(1)}, u32[]{:S(2)}, u32[]{:S(2)}) collective-permute-start(bf16[512,512]{0,1:T(8,128)(2,1)S(1)} %add_convert_fusion), channel_id=1, source_target_pairs={{16,0},{18,2},{20,4},{22,6},{24,8},{26,10},{28,12},{30,14},{32,16}... | collective-permute-start | bytes 1572872 | tf_op jit(solution)/shard_map/ppermute | solution.py:15
  111.8 10.9 %collective-permute-done.15 = bf16[512,512]{0,1:T(8,128)(2,1)S(1)} collective-permute-done((bf16[512,512]{0,1:T(8,128)(2,1)S(1)}, bf16[512,512]{0,1:T(8,128)(2,1)S(1)}, u32[]{:S(2)}, u32[]{:S(2)}) %collective-permute-start.15) | collective-permute-done | bytes 524320 | tf_op jit(solution)/shard_map/ppermute | solution.py:15
  123.1 1.8 convolution_bitcast_fusion
  124.9 1.0 copy-done.2
  128.0 1.0 copy.27
  129.0 285.0 %all-reduce.3.cloned.1.call-done = f32[768,512]{0,1:T(8,128)} async-done(((f32[768,512]{0,1:T(8,128)}), f32[768,512]{0,1:T(8,128)}) %all-reduce.3.cloned.1.call-update) | async-done | bytes 1572880
  414.1 1.2 constant_dynamic-slice_fusion
  415.2 0.7 copy.28
  (67 shorter events, 15.0 us)
Async XLA Ops:
  7.2 1.1 copy-start
  7.2 3.1 copy-start.5
  7.2 406.9 %all-reduce.3.cloned.1.call-start = ((), (), s32[]{:S(2)}) async-start(), calls=%async_computation | async-start | bytes 3145728
  10.2 8.8 %collective-permute-start = (bf16[512,512]{0,1:T(8,128)(2,1)S(1)}, bf16[512,512]{0,1:T(8,128)(2,1)}, u32[]{:S(2)}, u32[]{:S(2)}) collective-permute-start(bf16[512,512]{0,1:T(8,128)(2,1)S(1)} %multiply_convert_fusion.1), channel_id=1, source_target_pairs={{254,0},{0,2},{2,4},{4,6},{6,8},{8,10},{10,12},{12,14},{14,16},{16... | collective-permute-start | bytes 1572872 | tf_op jit(solution)/shard_map/ppermute | solution.py:15
  19.0 8.8 %collective-permute-start.1 = (bf16[512,512]{0,1:T(8,128)(2,1)}, bf16[512,512]{0,1:T(8,128)(2,1)S(1)}, u32[]{:S(2)}, u32[]{:S(2)}) collective-permute-start(bf16[512,512]{0,1:T(8,128)(2,1)} %collective-permute-done), channel_id=1, source_target_pairs={{254,0},{0,2},{2,4},{4,6},{6,8},{8,10},{10,12},{12,14},{14,16},{16... | collective-permute-start | bytes 1572872 | tf_op jit(solution)/shard_map/ppermute | solution.py:15
  21.1 12.3 %collective-permute-start.8 = (bf16[512,512]{0,1:T(8,128)(2,1)S(1)}, bf16[512,512]{0,1:T(8,128)(2,1)S(1)}, u32[]{:S(2)}, u32[]{:S(2)}) collective-permute-start(bf16[512,512]{0,1:T(8,128)(2,1)S(1)} %convolution_convert_fusion), channel_id=1, source_target_pairs={{254,0},{0,2},{2,4},{4,6},{6,8},{8,10},{10,12},{12,14},{14,16},{16... | collective-permute-start | bytes 1572872 | tf_op jit(solution)/shard_map/ppermute | solution.py:15
  27.8 11.2 %collective-permute-start.2 = (bf16[512,512]{0,1:T(8,128)(2,1)S(1)}, bf16[512,512]{0,1:T(8,128)(2,1)S(1)}, u32[]{:S(2)}, u32[]{:S(2)}) collective-permute-start(bf16[512,512]{0,1:T(8,128)(2,1)S(1)} %collective-permute-done.1), channel_id=1, source_target_pairs={{254,0},{0,2},{2,4},{4,6},{6,8},{8,10},{10,12},{12,14},{14,16},{16... | collective-permute-start | bytes 1572872 | tf_op jit(solution)/shard_map/ppermute | solution.py:15
  33.9 10.8 %collective-permute-start.9 = (bf16[512,512]{0,1:T(8,128)(2,1)S(1)}, bf16[512,512]{0,1:T(8,128)(2,1)S(1)}, u32[]{:S(2)}, u32[]{:S(2)}) collective-permute-start(bf16[512,512]{0,1:T(8,128)(2,1)S(1)} %add_convert_fusion.6), channel_id=1, source_target_pairs={{254,0},{0,2},{2,4},{4,6},{6,8},{8,10},{10,12},{12,14},{14,16},{16... | collective-permute-start | bytes 1572872 | tf_op jit(solution)/shard_map/ppermute | solution.py:15
  39.1 11.2 %collective-permute-start.3 = (bf16[512,512]{0,1:T(8,128)(2,1)S(1)}, bf16[512,512]{0,1:T(8,128)(2,1)S(1)}, u32[]{:S(2)}, u32[]{:S(2)}) collective-permute-start(bf16[512,512]{0,1:T(8,128)(2,1)S(1)} %collective-permute-done.2), channel_id=1, source_target_pairs={{254,0},{0,2},{2,4},{4,6},{6,8},{8,10},{10,12},{12,14},{14,16},{16... | collective-permute-start | bytes 1572872 | tf_op jit(solution)/shard_map/ppermute | solution.py:15
  44.8 11.1 %collective-permute-start.10 = (bf16[512,512]{0,1:T(8,128)(2,1)S(1)}, bf16[512,512]{0,1:T(8,128)(2,1)S(1)}, u32[]{:S(2)}, u32[]{:S(2)}) collective-permute-start(bf16[512,512]{0,1:T(8,128)(2,1)S(1)} %add_convert_fusion.5), channel_id=1, source_target_pairs={{254,0},{0,2},{2,4},{4,6},{6,8},{8,10},{10,12},{12,14},{14,16},{16... | collective-permute-start | bytes 1572872 | tf_op jit(solution)/shard_map/ppermute | solution.py:15
  50.3 11.2 %collective-permute-start.4 = (bf16[512,512]{0,1:T(8,128)(2,1)S(1)}, bf16[512,512]{0,1:T(8,128)(2,1)S(1)}, u32[]{:S(2)}, u32[]{:S(2)}) collective-permute-start(bf16[512,512]{0,1:T(8,128)(2,1)S(1)} %collective-permute-done.3), channel_id=1, source_target_pairs={{254,0},{0,2},{2,4},{4,6},{6,8},{8,10},{10,12},{12,14},{14,16},{16... | collective-permute-start | bytes 1572872 | tf_op jit(solution)/shard_map/ppermute | solution.py:15
  56.1 11.1 %collective-permute-start.11 = (bf16[512,512]{0,1:T(8,128)(2,1)S(1)}, bf16[512,512]{0,1:T(8,128)(2,1)S(1)}, u32[]{:S(2)}, u32[]{:S(2)}) collective-permute-start(bf16[512,512]{0,1:T(8,128)(2,1)S(1)} %add_convert_fusion.4), channel_id=1, source_target_pairs={{254,0},{0,2},{2,4},{4,6},{6,8},{8,10},{10,12},{12,14},{14,16},{16... | collective-permute-start | bytes 1572872 | tf_op jit(solution)/shard_map/ppermute | solution.py:15
  61.5 11.4 %collective-permute-start.5 = (bf16[512,512]{0,1:T(8,128)(2,1)S(1)}, bf16[512,512]{0,1:T(8,128)(2,1)S(1)}, u32[]{:S(2)}, u32[]{:S(2)}) collective-permute-start(bf16[512,512]{0,1:T(8,128)(2,1)S(1)} %collective-permute-done.4), channel_id=1, source_target_pairs={{254,0},{0,2},{2,4},{4,6},{6,8},{8,10},{10,12},{12,14},{14,16},{16... | collective-permute-start | bytes 1572872 | tf_op jit(solution)/shard_map/ppermute | solution.py:15
  67.3 12.5 %collective-permute-start.12 = (bf16[512,512]{0,1:T(8,128)(2,1)S(1)}, bf16[512,512]{0,1:T(8,128)(2,1)S(1)}, u32[]{:S(2)}, u32[]{:S(2)}) collective-permute-start(bf16[512,512]{0,1:T(8,128)(2,1)S(1)} %add_convert_fusion.3), channel_id=1, source_target_pairs={{254,0},{0,2},{2,4},{4,6},{6,8},{8,10},{10,12},{12,14},{14,16},{16... | collective-permute-start | bytes 1572872 | tf_op jit(solution)/shard_map/ppermute | solution.py:15
  72.9 12.8 %collective-permute-start.6 = (bf16[512,512]{0,1:T(8,128)(2,1)S(1)}, bf16[512,512]{0,1:T(8,128)(2,1)S(1)}, u32[]{:S(2)}, u32[]{:S(2)}) collective-permute-start(bf16[512,512]{0,1:T(8,128)(2,1)S(1)} %collective-permute-done.5), channel_id=1, source_target_pairs={{254,0},{0,2},{2,4},{4,6},{6,8},{8,10},{10,12},{12,14},{14,16},{16... | collective-permute-start | bytes 1572872 | tf_op jit(solution)/shard_map/ppermute | solution.py:15
  80.0 12.9 %collective-permute-start.13 = (bf16[512,512]{0,1:T(8,128)(2,1)S(1)}, bf16[512,512]{0,1:T(8,128)(2,1)S(1)}, u32[]{:S(2)}, u32[]{:S(2)}) collective-permute-start(bf16[512,512]{0,1:T(8,128)(2,1)S(1)} %add_convert_fusion.2), channel_id=1, source_target_pairs={{254,0},{0,2},{2,4},{4,6},{6,8},{8,10},{10,12},{12,14},{14,16},{16... | collective-permute-start | bytes 1572872 | tf_op jit(solution)/shard_map/ppermute | solution.py:15
  85.8 0.8 copy-start.6
  85.8 12.8 %collective-permute-start.7 = (bf16[512,512]{0,1:T(8,128)(2,1)S(1)}, bf16[512,512]{0,1:T(8,128)(2,1)S(1)}, u32[]{:S(2)}, u32[]{:S(2)}) collective-permute-start(bf16[512,512]{0,1:T(8,128)(2,1)S(1)} %collective-permute-done.6), channel_id=1, source_target_pairs={{254,0},{0,2},{2,4},{4,6},{6,8},{8,10},{10,12},{12,14},{14,16},{16... | collective-permute-start | bytes 1572872 | tf_op jit(solution)/shard_map/ppermute | solution.py:15
  86.6 0.8 copy-start.1
  93.1 12.9 %collective-permute-start.14 = (bf16[512,512]{0,1:T(8,128)(2,1)S(1)}, bf16[512,512]{0,1:T(8,128)(2,1)S(1)}, u32[]{:S(2)}, u32[]{:S(2)}) collective-permute-start(bf16[512,512]{0,1:T(8,128)(2,1)S(1)} %add_convert_fusion.1), channel_id=1, source_target_pairs={{254,0},{0,2},{2,4},{4,6},{6,8},{8,10},{10,12},{12,14},{14,16},{16... | collective-permute-start | bytes 1572872 | tf_op jit(solution)/shard_map/ppermute | solution.py:15
  98.6 0.8 copy-start.8
  99.4 0.8 copy-start.3
  106.1 16.5 %collective-permute-start.15 = (bf16[512,512]{0,1:T(8,128)(2,1)S(1)}, bf16[512,512]{0,1:T(8,128)(2,1)S(1)}, u32[]{:S(2)}, u32[]{:S(2)}) collective-permute-start(bf16[512,512]{0,1:T(8,128)(2,1)S(1)} %add_convert_fusion), channel_id=1, source_target_pairs={{16,0},{18,2},{20,4},{22,6},{24,8},{26,10},{28,12},{30,14},{32,16}... | collective-permute-start | bytes 1572872 | tf_op jit(solution)/shard_map/ppermute | solution.py:15
  124.9 1.0 copy-start.2
  124.9 1.2 copy-start.7
  126.1 1.0 copy-start.4
  126.1 1.2 copy-start.9
Sparse Core Ops, SparseCore 0:
  125.1 288.9 all-reduce.2
where the time goes:
time: 426 us; the launch traced here: 423 us
  waiting for transfers between devices  371 us (87%)
  matrix products  19.5 us (5%)
  between operations  15.7 us (4%)
  local copies, waits for them, and re-layouts  8.01 us (2%)
  starting transfers between devices  7.46 us (2%)
    unnamed x2, waiting for transfers between devices  285 us
    ppermute x16, waiting for transfers between devices, passed_along(): return lax.ppermute(block, axis, route)  85.6 us
  transfers between devices with their start and end apart: 17, of which 17 were waited for; matrix products, arithmetic and copies ran while one was open for 4% of the time, Pallas kernels for 0%

commit v1 on v0

v1 whole, which is shorter than its diff:
```python
import jax
import jax.numpy as jnp
from jax import lax
from jax.sharding import Mesh, PartitionSpec as P

EPS = 1e-06
SHIFTS = 8
PIECES = 2
AXES = ("x", "yl", "z", "c", "yh")
DP = ("x", "yl", "z", "c")
CHIPS = ("x", "yl", "z", "yh")
SIZES = (4, 2, 8, 2, 2)


def unit_rows(values):
    square = jnp.sum(values * values, axis=-1, keepdims=True)
    factor = lax.rsqrt(square + EPS)
    return (values * factor, factor)


def back_rows(normal, factor, upstream):
    return factor * (upstream - normal * jnp.sum(normal * upstream, axis=-1, keepdims=True))


def next_chip(block):
    chips = lax.axis_size(DP) // 2
    route = [(2 * i + c, 2 * ((i + (1, -1)[c]) % chips) + c) for i in range(chips) for c in (0, 1)]
    return lax.ppermute(block, DP, route)


def other_core(block):
    return lax.ppermute(block, "c", [(0, 1), (1, 0)])


def on_device(images, text_feats, text_proj, logit_scale, logit_bias):
    core = lax.axis_index("c")
    first = core == 0
    rows = images.shape[0]
    bf16, f32 = jnp.bfloat16, jnp.float32
    scaling, shifted = logit_scale[0], logit_bias[0]

    images_raw = images.astype(f32)
    text_raw = jnp.dot(text_feats, text_proj, preferred_element_type=f32)
    image_unit, image_factor = unit_rows(images_raw)
    text_unit, text_factor = unit_rows(text_raw)
    u_round = image_unit.astype(bf16)
    v_round = text_unit.astype(bf16)

    stream_own = jnp.where(first, v_round, u_round)
    still_own = jnp.where(first, u_round, v_round)
    stream_sib = other_core(still_own)
    raw_sib = other_core(jnp.where(first, text_raw, images_raw))
    feats_sib = other_core(text_feats)
    unit_own = jnp.where(first, image_unit, text_unit)
    factor_own = jnp.where(first, image_factor, text_factor)
    unit_sib, factor_sib = unit_rows(raw_sib)
    still_sib = unit_sib.astype(bf16)

    def weigh(still, held, row0):
        logits = (
            scaling
            * lax.dot_general(still, held, (((1,), (1,)), ((), ())), preferred_element_type=f32)
            + shifted
        )
        if row0 is None:
            return (scaling * jax.nn.sigmoid(logits)).astype(bf16)
        r = lax.broadcasted_iota(jnp.int32, logits.shape, 0)
        q = lax.broadcasted_iota(jnp.int32, logits.shape, 1) + row0
        label = jnp.where(r == q, 1.0, -1.0).astype(f32)
        return (scaling * -label * jax.nn.sigmoid(-label * logits)).astype(bf16)

    def term(still, held, row0=None):
        return jnp.dot(weigh(still, held, row0), held, preferred_element_type=f32)

    step = rows // PIECES
    cut = lambda b: [b[i * step : (i + 1) * step] for i in range(PIECES)]
    held_own, held_sib = cut(stream_own), cut(stream_sib)
    moving_own = [next_chip(b) for b in held_own]
    moving_sib = [next_chip(b) for b in held_sib]
    sum_own = sum_sib = 0.0
    for i in range(PIECES):
        sum_own = sum_own + term(still_own, held_own[i], i * step)
        sum_sib = sum_sib + term(still_sib, held_own[i])
    for i in range(PIECES):
        sum_sib = sum_sib + term(still_sib, held_sib[i], i * step)
    last = SHIFTS // 2
    for hop in range(1, last + 1):
        held_own, held_sib = moving_own, moving_sib
        if hop < last:
            moving_own = [next_chip(b) for b in held_own]
            moving_sib = [next_chip(b) for b in held_sib]
        for b in held_own:
            sum_own = sum_own + term(still_own, b)
            if hop < last:
                sum_sib = sum_sib + term(still_sib, b)
        for b in held_sib:
            sum_own = sum_own + term(still_own, b)
            sum_sib = sum_sib + term(still_sib, b)

    grads = jnp.concatenate(
        [back_rows(unit_own, factor_own, sum_own), back_rows(unit_sib, factor_sib, sum_sib)]
    ).astype(bf16)
    crossed = other_core(grads)
    image_grad = jnp.where(first, grads[:rows], crossed[rows:])
    text_grads = jnp.where(first, crossed, grads)
    feats = jnp.concatenate(
        [jnp.where(first, feats_sib, text_feats), jnp.where(first, text_feats, feats_sib)]
    )

    chips = 128
    wide = text_feats.shape[1]
    per = wide // (2 * chips)
    at = lax.broadcasted_iota(jnp.int32, (wide, per * chips), 1)
    chip, j = at % chips, at // chips
    owner = (chip // 2) * 4 + core * 2 + chip % 2
    pick = (lax.broadcasted_iota(jnp.int32, (wide, per * chips), 0) == owner * per + j).astype(bf16)
    picked = jnp.dot(feats, pick, preferred_element_type=f32).astype(bf16)
    part = lax.dot_general(picked, text_grads, (((0,), (0,)), ((), ())), preferred_element_type=f32)
    part = part.astype(bf16).reshape(per, chips, -1)
    spread = lax.all_to_all(part, CHIPS, 1, 0, tiled=True)
    proj_grad = jnp.sum(spread.reshape(chips, per, -1).astype(f32), axis=0)
    return (image_grad, proj_grad)


def solution(mesh):
    fine = Mesh(mesh.devices.reshape(SIZES), AXES)
    split = P(AXES, None)
    in_specs = (split, split, P(), P(), P())
    return jax.shard_map(
        on_device, mesh=fine, in_specs=in_specs, out_specs=(split, split), check_vma=False
    )
```

time: 426 us -> 211 us (0.50)
  waiting for transfers between devices: 371 us -> 25.7 us
  matrix products: 19.5 us -> 115 us
  starting transfers between devices: 7.46 us -> 49.2 us
  between operations: 15.7 us -> 2.31 us
  other arithmetic: 1.45 us -> 8.43 us
    unnamed x2 -> x0, waiting for transfers between devices: 285 us -> none
    dot_general x29 -> x38, matrix products: 19.5 us -> 115 us  [the longest x36 110 us: term(): return jnp.dot(weigh(still, held, row0), held, preferred_element_type=f32)]
    ppermute x16 -> x20, waiting for transfers between devices: 85.6 us -> 8.15 us  [the longest x16 5.96 us: next_chip(): return lax.ppermute(block, DP, route)]
    ppermute x16 -> x20, starting transfers between devices: 7.43 us -> 37.9 us  [the longest x16 32.1 us: next_chip(): return lax.ppermute(block, DP, route)]
    all_to_all x0 -> x1, waiting for transfers between devices: none -> 17.6 us  [on_device(): spread = lax.all_to_all(part, CHIPS, 1, 0, tiled=True)]
    all_to_all x0 -> x1, starting transfers between devices: none -> 11.3 us  [on_device(): spread = lax.all_to_all(part, CHIPS, 1, 0, tiled=True)]
    unnamed x24 -> x6, local copies, waits for them, and re-layouts: 8.01 us -> 2.35 us
    select_n x0 -> x5, other arithmetic: none -> 5.52 us  [the longest x1 2.64 us: on_device(): jnp.where(first, feats_sib, text_feats)]
  transfers between devices with their start and end apart: 17 -> 21, of which waited for: 17 -> 5; matrix products, arithmetic and copies ran while one was open for 4% -> 56% of each run, Pallas kernels for 0% -> 0%
where the time goes in v1:
time: 211 us; the launch traced here: 207 us
  matrix products  115 us (55%)
  starting transfers between devices  49.2 us (23%)
  waiting for transfers between devices  25.7 us (12%)
  other arithmetic  8.43 us (4%)
  local copies, waits for them, and re-layouts  6.23 us (3%)
  between operations  2.31 us (1%)
    dot_general x36, matrix products, term(): return jnp.dot(weigh(still, held, row0), held, preferred_element_type=f32)  110 us
    ppermute x16, starting transfers between devices, next_chip(): return lax.ppermute(block, DP, route)  32.1 us
    all_to_all x1, waiting for transfers between devices, on_device(): spread = lax.all_to_all(part, CHIPS, 1, 0, tiled=True)  17.6 us
    all_to_all x1, starting transfers between devices, on_device(): spread = lax.all_to_all(part, CHIPS, 1, 0, tiled=True)  11.3 us
    ppermute x16, waiting for transfers between devices, next_chip(): return lax.ppermute(block, DP, route)  5.96 us
    ppermute x4, starting transfers between devices, other_core(): return lax.ppermute(block, 'c', [(0, 1), (1, 0)])  5.85 us
  transfers between devices with their start and end apart: 21, of which 5 were waited for; matrix products, arithmetic and copies ran while one was open for 56% of the time, Pallas kernels for 0%

profile of v1, /device:TPU:32, one launch (start us, length us, event | category | flops | bytes accessed | tf_op | source)
XLA Modules:
  0.0 207.0 jit_solution(16662258746299895460)
XLA Ops:
  12.0 3.0 %convolution_add_fusion.9 = f32[512,512]{0,1:T(8,128)} fusion(f32[512,512]{0,1:T(8,128)} %fusion.305, bf16[512,512]{0,1:T(8,128)(2,1)S(1)} %get-tuple-element.7, s32[256]{0:T(256)S(1)} %iota_add_fusion, f32[]{:T(128)} %bitcast.172, f32[]{:T(128)} %bitcast.134, bf16[512,512]{0,1:T(8,128)(2,1)S(1)} %get-tuple-element.6), kind=kOutput, calls=%fused_computation.33 | convolution fusion | flops 270270464 | bytes 3146760 | tf_op jit(solution)/shard_map/dot_general | solution.py:73
  15.0 3.1 %collective-permute-start.6 = (bf16[256,512]{0,1:T(8,128)(2,1)}, bf16[256,512]{0,1:T(8,128)(2,1)}, u32[]{:S(2)}, u32[]{:S(2)}) collective-permute-start(bf16[256,512]{0,1:T(8,128)(2,1)} %collective-permute-done.1), channel_id=1, source_target_pairs={{0,4},{2,254},{4,8},{6,2},{8,12},{10,6},{12,16},{14,10},{16,20},{1... | collective-permute-start | bytes 786440 | tf_op jit(solution)/shard_map/ppermute | solution.py:28
  19.2 2.8 %fusion.329 = f32[512,512]{0,1:T(8,128)} fusion(bf16[256,512]{0,1:T(8,128)(2,1)} %collective-permute-done.1, bf16[512,512]{0,1:T(8,128)(2,1)S(1)} %get-tuple-element.7, f32[]{:T(128)} %bitcast.170, f32[]{:T(128)} %bitcast.130), kind=kOutput, calls=%fused_computation.383 | convolution fusion | flops 269352960 | bytes 1835016 | tf_op jit(solution)/shard_map/dot_general | solution.py:73
  28.3 2.8 %fusion.326 = f32[512,512]{0,1:T(8,128)} fusion(bf16[256,512]{0,1:T(8,128)(2,1)} %collective-permute-done.6, bf16[512,512]{0,1:T(8,128)(2,1)S(1)} %get-tuple-element.7, f32[]{:T(128)} %bitcast.166, f32[]{:T(128)} %bitcast.122), kind=kOutput, calls=%fused_computation.380 | convolution fusion | flops 269352960 | bytes 1835016 | tf_op jit(solution)/shard_map/dot_general | solution.py:73
  40.0 2.8 %fusion.327 = f32[512,512]{0,1:T(8,128)} fusion(bf16[256,512]{0,1:T(8,128)(2,1)} %collective-permute-done.4, bf16[512,512]{0,1:T(8,128)(2,1)S(1)} %get-tuple-element.7, f32[]{:T(128)} %bitcast.168, f32[]{:T(128)} %bitcast.126), kind=kOutput, calls=%fused_computation.381 | convolution fusion | flops 269352960 | bytes 1835016 | tf_op jit(solution)/shard_map/dot_general | solution.py:73
  45.6 4.1 %fusion.16 = f32[512,512]{0,1:T(8,128)} fusion(f32[512,512]{0,1:T(8,128)} %fusion.327, f32[512,512]{0,1:T(8,128)} %fusion.328, f32[512,512]{0,1:T(8,128)} %fusion.329, f32[512,512]{0,1:T(8,128)} %convolution_add_fusion.9, bf16[256,512]{0,1:T(8,128)(2,1)} %collective-permute-done, bf16[512,512]{0,1:T(8,128)(2,1)S(1)} %get-tuple-element.7, f32[]{:T(128)} %bitcast.171, ...), kind=kOutput, calls=%fused_computation.35 | convolution fusion | flops 270401536 | bytes 6029320 | tf_op jit(solution)/shard_map/dot_general | solution.py:73
  49.7 2.8 %fusion.323 = f32[512,512]{0,1:T(8,128)} fusion(bf16[256,512]{0,1:T(8,128)(2,1)} %collective-permute-done.10, bf16[512,512]{0,1:T(8,128)(2,1)S(1)} %get-tuple-element.7, f32[]{:T(128)} %bitcast.162, f32[]{:T(128)} %bitcast.114), kind=kOutput, calls=%fused_computation.377 | convolution fusion | flops 269352960 | bytes 1835016 | tf_op jit(solution)/shard_map/dot_general | solution.py:73
  61.7 3.9 %fusion.18 = f32[512,512]{0,1:T(8,128)} fusion(f32[512,512]{0,1:T(8,128)} %fusion.324, f32[512,512]{0,1:T(8,128)} %fusion.325, f32[512,512]{0,1:T(8,128)} %fusion.326, f32[512,512]{0,1:T(8,128)} %fusion.16, bf16[256,512]{0,1:T(8,128)(2,1)S(1)} %collective-permute-done.5, bf16[512,512]{0,1:T(8,128)(2,1)S(1)} %get-tuple-element.7, f32[]{:T(128)} %bitcast.167, ...), kind=kOutput, calls=%fused_computation.37 | convolution fusion | flops 270401536 | bytes 6029320 | tf_op jit(solution)/shard_map/dot_general | solution.py:73
  65.6 2.8 %fusion.320 = f32[512,512]{0,1:T(8,128)} fusion(bf16[256,512]{0,1:T(8,128)(2,1)} %collective-permute-done.14, bf16[512,512]{0,1:T(8,128)(2,1)S(1)} %get-tuple-element.7, f32[]{:T(128)} %bitcast.158, f32[]{:T(128)} %bitcast.106), kind=kOutput, calls=%fused_computation.374 | convolution fusion | flops 269352960 | bytes 1835016 | tf_op jit(solution)/shard_map/dot_general | solution.py:73
  68.5 12.9 %collective-permute-start.16 = (bf16[256,512]{0,1:T(8,128)(2,1)}, bf16[256,512]{0,1:T(8,128)(2,1)}, u32[]{:S(2)}, u32[]{:S(2)}) collective-permute-start(bf16[256,512]{0,1:T(8,128)(2,1)} %collective-permute-done.12), channel_id=1, source_target_pairs={{0,4},{2,254},{4,8},{6,2},{8,12},{10,6},{12,16},{14,10},{16,20},{1... | collective-permute-start | bytes 786440 | tf_op jit(solution)/shard_map/ppermute | solution.py:28
  81.4 2.8 %fusion.321 = f32[512,512]{0,1:T(8,128)} fusion(bf16[256,512]{0,1:T(8,128)(2,1)} %collective-permute-done.12, bf16[512,512]{0,1:T(8,128)(2,1)S(1)} %get-tuple-element.7, f32[]{:T(128)} %bitcast.160, f32[]{:T(128)} %bitcast.110), kind=kOutput, calls=%fused_computation.375 | convolution fusion | flops 269352960 | bytes 1835016 | tf_op jit(solution)/shard_map/dot_general | solution.py:73
  87.0 3.9 %fusion.20 = f32[512,512]{0,1:T(8,128)} fusion(f32[512,512]{0,1:T(8,128)} %fusion.321, f32[512,512]{0,1:T(8,128)} %fusion.322, f32[512,512]{0,1:T(8,128)} %fusion.323, f32[512,512]{0,1:T(8,128)} %fusion.18, bf16[256,512]{0,1:T(8,128)(2,1)S(1)} %collective-permute-done.9, bf16[512,512]{0,1:T(8,128)(2,1)S(1)} %get-tuple-element.7, f32[]{:T(128)} %bitcast.163, ...), kind=kOutput, calls=%fused_computation.39 | convolution fusion | flops 270401536 | bytes 6029320 | tf_op jit(solution)/shard_map/dot_general | solution.py:73
  90.9 2.8 %fusion.319 = f32[512,512]{0,1:T(8,128)} fusion(bf16[256,512]{0,1:T(8,128)(2,1)} %collective-permute-done.15, bf16[512,512]{0,1:T(8,128)(2,1)S(1)} %get-tuple-element.7, f32[]{:T(128)} %bitcast.157, f32[]{:T(128)} %bitcast.104), kind=kOutput, calls=%fused_computation.373 | convolution fusion | flops 269352960 | bytes 1835016 | tf_op jit(solution)/shard_map/dot_general | solution.py:73
  96.5 4.2 %multiply_reduce_fusion.2 = (f32[512]{0:T(512)S(1)}, f32[512,512]{0,1:T(8,128)}) fusion(f32[512,512]{0,1:T(8,128)S(1)} %get-tuple-element.20, bf16[512,512]{0,1:T(8,128)(2,1)S(1)} %copy.45, f32[512]{0:T(512)S(1)} %get-tuple-element.17, f32[512]{0:T(512)S(1)} %get-tuple-element.18, pred[]{:T(512)S(6)} %eq.25, f32[512,512]{0,1:T(8,128)} %fusion.318, ...), kind=kOutput, calls=%fused_computation.392 | convolution fusion | flops 271973888 | bytes 7608329 | tf_op jit(solution)/shard_map/dot_general | solution.py:73
  102.3 5.0 %collective-permute-start.17 = (f32[512,512]{0,1:T(8,128)S(1)}, f32[512,512]{0,1:T(8,128)S(1)}, u32[]{:S(2)}, u32[]{:S(2)}) collective-permute-start(f32[512,512]{0,1:T(8,128)S(1)} %get-tuple-element.10), channel_id=1, source_target_pairs={{0,2},{2,0},{1,3},{3,1},{4,6},{6,4},{5,7},{7,5},{8,10},{10,8},{9,1... | collective-permute-start | bytes 3145736 | tf_op jit(solution)/shard_map/ppermute | solution.py:32
  109.8 2.8 %fusion.317 = f32[512,512]{0,1:T(8,128)} fusion(bf16[512,512]{0,1:T(8,128)(2,1)S(1)} %multiply_convert_fusion.3, f32[]{:T(128)} %bitcast.155, f32[]{:T(128)} %bitcast.135, bf16[512,512]{0,1:T(8,128)(2,1)} %copy-done.1), kind=kOutput, calls=%fused_computation.371 | convolution fusion | flops 269352960 | bytes 2097160 | tf_op jit(solution)/shard_map/dot_general | solution.py:73
  112.6 3.2 %convolution_add_fusion.4 = f32[512,512]{0,1:T(8,128)} fusion(f32[512,512]{0,1:T(8,128)} %fusion.317, bf16[512,512]{0,1:T(8,128)(2,1)S(1)} %multiply_convert_fusion.3, f32[]{:T(128)} %bitcast.154, f32[]{:T(128)} %bitcast.131, bf16[512,512]{0,1:T(8,128)(2,1)} %copy-done.1), kind=kOutput, calls=%fused_computation.24 | convolution fusion | flops 269615104 | bytes 3145736 | tf_op jit(solution)/shard_map/dot_general | solution.py:73
  124.1 2.8 %fusion.316 = f32[512,512]{0,1:T(8,128)} fusion(bf16[256,512]{0,1:T(8,128)(2,1)} %collective-permute-done, bf16[512,512]{0,1:T(8,128)(2,1)S(1)} %multiply_convert_fusion.3, f32[]{:T(128)} %bitcast.151, f32[]{:T(128)} %bitcast.123), kind=kOutput, calls=%fused_computation.370 | convolution fusion | flops 269352960 | bytes 1835016 | tf_op jit(solution)/shard_map/dot_general | solution.py:73
  126.9 2.9 %fusion.304 = f32[512,512]{0,1:T(8,128)} fusion(bf16[512,512]{0,1:T(8,128)(2,1)S(1)} %multiply_convert_fusion.3, s32[256]{0:T(256)S(1)} %iota_add_fusion, f32[]{:T(128)} %bitcast.152, f32[]{:T(128)} %bitcast.127, bf16[512,512]{0,1:T(8,128)(2,1)} %collective-permute-done.2), kind=kOutput, calls=%fused_computation.358 | convolution fusion | flops 270008320 | bytes 2098184 | tf_op jit(solution)/shard_map/dot_general | solution.py:73
  129.8 2.8 %fusion.311 = f32[512,512]{0,1:T(8,128)} fusion(bf16[256,512]{0,1:T(8,128)(2,1)} %collective-permute-done.7, bf16[512,512]{0,1:T(8,128)(2,1)S(1)} %multiply_convert_fusion.3, f32[]{:T(128)} %bitcast.145, f32[]{:T(128)} %bitcast.133), kind=kOutput, calls=%fused_computation.365 | convolution fusion | flops 269352960 | bytes 1835016 | tf_op jit(solution)/shard_map/dot_general | solution.py:73
  135.4 2.9 %fusion.312 = f32[512,512]{0,1:T(8,128)} fusion(bf16[256,512]{0,1:T(8,128)(2,1)} %collective-permute-done.6, bf16[512,512]{0,1:T(8,128)(2,1)S(1)} %multiply_convert_fusion.3, f32[]{:T(128)} %bitcast.146, f32[]{:T(128)} %bitcast.103), kind=kOutput, calls=%fused_computation.366 | convolution fusion | flops 269352960 | bytes 1835016 | tf_op jit(solution)/shard_map/dot_general | solution.py:73
  138.2 2.8 %fusion.309 = f32[512,512]{0,1:T(8,128)} fusion(bf16[256,512]{0,1:T(8,128)(2,1)} %collective-permute-done.10, bf16[512,512]{0,1:T(8,128)(2,1)S(1)} %multiply_convert_fusion.3, f32[]{:T(128)} %bitcast.142, f32[]{:T(128)} %bitcast.105), kind=kOutput, calls=%fused_computation.363 | convolution fusion | flops 269352960 | bytes 1835016 | tf_op jit(solution)/shard_map/dot_general | solution.py:73
  141.0 2.8 %fusion.308 = f32[512,512]{0,1:T(8,128)} fusion(bf16[256,512]{0,1:T(8,128)(2,1)} %collective-permute-done.11, bf16[512,512]{0,1:T(8,128)(2,1)S(1)} %multiply_convert_fusion.3, f32[]{:T(128)} %bitcast.141, f32[]{:T(128)} %bitcast.125), kind=kOutput, calls=%fused_computation.362 | convolution fusion | flops 269352960 | bytes 1835016 | tf_op jit(solution)/shard_map/dot_general | solution.py:73
  143.8 2.8 %fusion.307 = f32[512,512]{0,1:T(8,128)} fusion(bf16[256,512]{0,1:T(8,128)(2,1)} %collective-permute-done.12, bf16[512,512]{0,1:T(8,128)(2,1)S(1)} %multiply_convert_fusion.3, f32[]{:T(128)} %bitcast.140, f32[]{:T(128)} %bitcast.109), kind=kOutput, calls=%fused_computation.361 | convolution fusion | flops 269352960 | bytes 1835016 | tf_op jit(solution)/shard_map/dot_general | solution.py:73
  146.6 2.8 %fusion.306 = f32[512,512]{0,1:T(8,128)} fusion(bf16[256,512]{0,1:T(8,128)(2,1)} %collective-permute-done.16, bf16[512,512]{0,1:T(8,128)(2,1)S(1)} %multiply_convert_fusion.3, f32[]{:T(128)} %bitcast.138, f32[]{:T(128)} %bitcast.101), kind=kOutput, calls=%fused_computation.360 | convolution fusion | flops 269352960 | bytes 1835016 | tf_op jit(solution)/shard_map/dot_general | solution.py:73
  149.4 4.8 %fusion.26 = f32[512,512]{0,1:T(8,128)} fusion(f32[512,512]{0,1:T(8,128)} %fusion.313, f32[512,512]{0,1:T(8,128)} %fusion.314, f32[512,512]{0,1:T(8,128)} %fusion.315, f32[512,512]{0,1:T(8,128)} %fusion.316, f32[512,512]{0,1:T(8,128)} %fusion.304, f32[512,512]{0,1:T(8,128)} %convolution_add_fusion.4, bf16[512,512]{0,1:T(8,128)(2,1)S(1)} %multiply_convert_fusion.3, ...), kind=kOutput, calls=%fused_computation.45 | convolution fusion | flops 271581184 | bytes 8388616 | tf_op jit(solution)/shard_map/dot_general | solution.py:73
  154.2 3.9 %fusion.28 = f32[512,512]{0,1:T(8,128)} fusion(f32[512,512]{0,1:T(8,128)} %fusion.310, f32[512,512]{0,1:T(8,128)} %fusion.311, f32[512,512]{0,1:T(8,128)} %fusion.312, f32[512,512]{0,1:T(8,128)} %fusion.26, bf16[256,512]{0,1:T(8,128)(2,1)S(1)} %collective-permute-done.5, bf16[512,512]{0,1:T(8,128)(2,1)S(1)} %multiply_convert_fusion.3, f32[]{:T(128)} %bitcast.147, ...), kind=kOutput, calls=%fused_computation.47 | convolution fusion | flops 270401536 | bytes 6029320 | tf_op jit(solution)/shard_map/dot_general | solution.py:73
  158.2 3.9 %fusion.30 = f32[512,512]{0,1:T(8,128)} fusion(f32[512,512]{0,1:T(8,128)} %fusion.307, f32[512,512]{0,1:T(8,128)} %fusion.308, f32[512,512]{0,1:T(8,128)} %fusion.309, f32[512,512]{0,1:T(8,128)} %fusion.28, bf16[256,512]{0,1:T(8,128)(2,1)S(1)} %collective-permute-done.9, bf16[512,512]{0,1:T(8,128)(2,1)S(1)} %multiply_convert_fusion.3, f32[]{:T(128)} %bitcast.143, ...), kind=kOutput, calls=%fused_computation.49 | convolution fusion | flops 270401536 | bytes 6029320 | tf_op jit(solution)/shard_map/dot_general | solution.py:73
  162.1 3.5 %multiply_reduce_fusion = (f32[512]{0:T(512)S(1)}, f32[512,512]{0,1:T(8,128)}) fusion(f32[512,512]{0,1:T(8,128)S(1)} %collective-permute-done.17, f32[512]{0:T(512)S(1)} %add_rsqrt_fusion, f32[512,512]{0,1:T(8,128)} %fusion.306, f32[512,512]{0,1:T(8,128)} %fusion.30, bf16[256,512]{0,1:T(8,128)(2,1)} %collective-permute-done.15, ...), kind=kOutput, calls=%fused_computation.389 | convolution fusion | flops 270663168 | bytes 4984840 | tf_op jit(solution)/shard_map/dot_general | solution.py:73
  170.6 3.1 %convolution_convert_fusion = bf16[384,512]{1,0:T(8,128)(2,1)S(1)} fusion(bf16[512,768]{1,0:T(8,128)(2,1)} %get-tuple-element.9, bf16[512,768]{1,0:T(8,128)(2,1)} %get-tuple-element.8, bf16[1024,512]{0,1:T(8,128)(2,1)} %collective-permute-done.18, pred[]{:T(512)S(6)} %eq.25, s32[384]{0:T(512)S(1)} %get-tuple-element.25, s32[384]{0:T(512)S(1)} %get-tuple-element.28, ...), kind=kOutput, calls=%fused_computation.50 | convolution fusion | flops 1020952576 | bytes 4070149 | tf_op jit(solution)/shard_map/dot_general | solution.py:118
  174.9 11.3 %all-to-all-start = ((bf16[3,128,512]{2,0,1:T(4,128)(2,1)}), bf16[3,128,512]{2,0,1:T(4,128)(2,1)S(1)}, u32[]{:S(2)}, u32[]{:S(2)}) async-start(bf16[3,128,512]{2,0,1:T(4,128)(2,1)} %copy.82), calls=%async_computation | async-start | bytes 1048576 | tf_op jit(solution)/shard_map/all_to_all | solution.py:120
  188.3 17.6 %all-to-all-done = bf16[3,128,512]{2,0,1:T(4,128)(2,1)S(1)} async-done(((bf16[3,128,512]{2,0,1:T(4,128)(2,1)}), bf16[3,128,512]{2,0,1:T(4,128)(2,1)S(1)}, u32[]{:S(2)}, u32[]{:S(2)}) %all-to-all-start) | async-done | bytes 393248 | tf_op jit(solution)/shard_map/all_to_all | solution.py:120
  (73 shorter events, 68.2 us)
Async XLA Ops:
  0.6 1.5 copy-start
  4.2 7.9 %copy-start.1 = (bf16[512,512]{0,1:T(8,128)(2,1)}, bf16[512,512]{0,1:T(8,128)(2,1)S(1)}, u32[]{:S(2)}) copy-start(bf16[512,512]{0,1:T(8,128)(2,1)S(1)} %get-tuple-element.6) | copy-start | bytes 1572868
  4.2 17.8 %collective-permute-start.2 = (bf16[512,512]{0,1:T(8,128)(2,1)S(1)}, bf16[512,512]{0,1:T(8,128)(2,1)}, u32[]{:S(2)}, u32[]{:S(2)}) collective-permute-start(bf16[512,512]{0,1:T(8,128)(2,1)S(1)} %get-tuple-element.7), channel_id=1, source_target_pairs={{0,2},{2,0},{1,3},{3,1},{4,6},{6,4},{5,7},{7,5},{8,10},{10,8},{9,1... | collective-permute-start | bytes 1572872 | tf_op jit(solution)/shard_map/ppermute | solution.py:32
  5.1 9.9 %collective-permute-start.1 = (bf16[256,512]{0,1:T(8,128)(2,1)}, bf16[256,512]{0,1:T(8,128)(2,1)}, u32[]{:S(2)}, u32[]{:S(2)}) collective-permute-start(bf16[256,512]{0,1:T(8,128)(2,1)} %get-tuple-element.13), channel_id=1, source_target_pairs={{0,4},{2,254},{4,8},{6,2},{8,12},{10,6},{12,16},{14,10},{16,20},{1... | collective-permute-start | bytes 786440 | tf_op jit(solution)/shard_map/ppermute | solution.py:28
  7.0 11.1 %collective-permute-start = (bf16[256,512]{0,1:T(8,128)(2,1)}, bf16[256,512]{0,1:T(8,128)(2,1)}, u32[]{:S(2)}, u32[]{:S(2)}) collective-permute-start(bf16[256,512]{0,1:T(8,128)(2,1)} %get-tuple-element.12), channel_id=1, source_target_pairs={{0,4},{2,254},{4,8},{6,2},{8,12},{10,6},{12,16},{14,10},{16,20},{1... | collective-permute-start | bytes 786440 | tf_op jit(solution)/shard_map/ppermute | solution.py:28
  15.0 12.4 %collective-permute-start.6 = (bf16[256,512]{0,1:T(8,128)(2,1)}, bf16[256,512]{0,1:T(8,128)(2,1)}, u32[]{:S(2)}, u32[]{:S(2)}) collective-permute-start(bf16[256,512]{0,1:T(8,128)(2,1)} %collective-permute-done.1), channel_id=1, source_target_pairs={{0,4},{2,254},{4,8},{6,2},{8,12},{10,6},{12,16},{14,10},{16,20},{1... | collective-permute-start | bytes 786440 | tf_op jit(solution)/shard_map/ppermute | solution.py:28
  18.2 9.3 %collective-permute-start.5 = (bf16[256,512]{0,1:T(8,128)(2,1)}, bf16[256,512]{0,1:T(8,128)(2,1)S(1)}, u32[]{:S(2)}, u32[]{:S(2)}) collective-permute-start(bf16[256,512]{0,1:T(8,128)(2,1)} %collective-permute-done), channel_id=1, source_target_pairs={{0,4},{2,254},{4,8},{6,2},{8,12},{10,6},{12,16},{14,10},{16,20},{1... | collective-permute-start | bytes 786440 | tf_op jit(solution)/shard_map/ppermute | solution.py:28
  23.8 7.3 %collective-permute-start.4 = (bf16[256,512]{0,1:T(8,128)(2,1)}, bf16[256,512]{0,1:T(8,128)(2,1)}, u32[]{:S(2)}, u32[]{:S(2)}) collective-permute-start(bf16[256,512]{0,1:T(8,128)(2,1)} %get-tuple-element.15), channel_id=1, source_target_pairs={{0,4},{2,254},{4,8},{6,2},{8,12},{10,6},{12,16},{14,10},{16,20},{1... | collective-permute-start | bytes 786440 | tf_op jit(solution)/shard_map/ppermute | solution.py:28
  24.9 9.1 %collective-permute-start.3 = (bf16[256,512]{0,1:T(8,128)(2,1)}, bf16[256,512]{0,1:T(8,128)(2,1)}, u32[]{:S(2)}, u32[]{:S(2)}) collective-permute-start(bf16[256,512]{0,1:T(8,128)(2,1)} %get-tuple-element.14), channel_id=1, source_target_pairs={{0,4},{2,254},{4,8},{6,2},{8,12},{10,6},{12,16},{14,10},{16,20},{1... | collective-permute-start | bytes 786440 | tf_op jit(solution)/shard_map/ppermute | solution.py:28
  27.5 9.3 %collective-permute-start.10 = (bf16[256,512]{0,1:T(8,128)(2,1)}, bf16[256,512]{0,1:T(8,128)(2,1)}, u32[]{:S(2)}, u32[]{:S(2)}) collective-permute-start(bf16[256,512]{0,1:T(8,128)(2,1)} %collective-permute-done.6), channel_id=1, source_target_pairs={{0,4},{2,254},{4,8},{6,2},{8,12},{10,6},{12,16},{14,10},{16,20},{1... | collective-permute-start | bytes 786440 | tf_op jit(solution)/shard_map/ppermute | solution.py:28
  27.5 11.9 %collective-permute-start.9 = (bf16[256,512]{0,1:T(8,128)(2,1)S(1)}, bf16[256,512]{0,1:T(8,128)(2,1)S(1)}, u32[]{:S(2)}, u32[]{:S(2)}) collective-permute-start(bf16[256,512]{0,1:T(8,128)(2,1)S(1)} %collective-permute-done.5), channel_id=1, source_target_pairs={{0,4},{2,254},{4,8},{6,2},{8,12},{10,6},{12,16},{14,10},{16,20},{1... | collective-permute-start | bytes 786440 | tf_op jit(solution)/shard_map/ppermute | solution.py:28
  31.1 21.4 %collective-permute-start.8 = (bf16[256,512]{0,1:T(8,128)(2,1)}, bf16[256,512]{0,1:T(8,128)(2,1)}, u32[]{:S(2)}, u32[]{:S(2)}) collective-permute-start(bf16[256,512]{0,1:T(8,128)(2,1)} %collective-permute-done.4), channel_id=1, source_target_pairs={{0,4},{2,254},{4,8},{6,2},{8,12},{10,6},{12,16},{14,10},{16,20},{1... | collective-permute-start | bytes 786440 | tf_op jit(solution)/shard_map/ppermute | solution.py:28
  33.9 21.0 %collective-permute-start.7 = (bf16[256,512]{0,1:T(8,128)(2,1)}, bf16[256,512]{0,1:T(8,128)(2,1)}, u32[]{:S(2)}, u32[]{:S(2)}) collective-permute-start(bf16[256,512]{0,1:T(8,128)(2,1)} %collective-permute-done.3), channel_id=1, source_target_pairs={{0,4},{2,254},{4,8},{6,2},{8,12},{10,6},{12,16},{14,10},{16,20},{1... | collective-permute-start | bytes 786440 | tf_op jit(solution)/shard_map/ppermute | solution.py:28
  36.7 28.9 %collective-permute-start.14 = (bf16[256,512]{0,1:T(8,128)(2,1)}, bf16[256,512]{0,1:T(8,128)(2,1)}, u32[]{:S(2)}, u32[]{:S(2)}) collective-permute-start(bf16[256,512]{0,1:T(8,128)(2,1)} %collective-permute-done.10), channel_id=1, source_target_pairs={{0,4},{2,254},{4,8},{6,2},{8,12},{10,6},{12,16},{14,10},{16,20},{1... | collective-permute-start | bytes 786440 | tf_op jit(solution)/shard_map/ppermute | solution.py:28
  39.4 57.1 %collective-permute-start.13 = (bf16[256,512]{0,1:T(8,128)(2,1)S(1)}, bf16[256,512]{0,1:T(8,128)(2,1)}, u32[]{:S(2)}, u32[]{:S(2)}) collective-permute-start(bf16[256,512]{0,1:T(8,128)(2,1)S(1)} %collective-permute-done.9), channel_id=1, source_target_pairs={{0,4},{2,254},{4,8},{6,2},{8,12},{10,6},{12,16},{14,10},{16,20},{1... | collective-permute-start | bytes 786440 | tf_op jit(solution)/shard_map/ppermute | solution.py:28
  52.5 16.0 %collective-permute-start.12 = (bf16[256,512]{0,1:T(8,128)(2,1)}, bf16[256,512]{0,1:T(8,128)(2,1)}, u32[]{:S(2)}, u32[]{:S(2)}) collective-permute-start(bf16[256,512]{0,1:T(8,128)(2,1)} %collective-permute-done.8), channel_id=1, source_target_pairs={{0,4},{2,254},{4,8},{6,2},{8,12},{10,6},{12,16},{14,10},{16,20},{1... | collective-permute-start | bytes 786440 | tf_op jit(solution)/shard_map/ppermute | solution.py:28
  55.0 13.5 %collective-permute-start.11 = (bf16[256,512]{0,1:T(8,128)(2,1)}, bf16[256,512]{0,1:T(8,128)(2,1)}, u32[]{:S(2)}, u32[]{:S(2)}) collective-permute-start(bf16[256,512]{0,1:T(8,128)(2,1)} %collective-permute-done.7), channel_id=1, source_target_pairs={{0,4},{2,254},{4,8},{6,2},{8,12},{10,6},{12,16},{14,10},{16,20},{1... | collective-permute-start | bytes 786440 | tf_op jit(solution)/shard_map/ppermute | solution.py:28
  68.4 22.5 %collective-permute-start.15 = (bf16[256,512]{0,1:T(8,128)(2,1)}, bf16[256,512]{0,1:T(8,128)(2,1)}, u32[]{:S(2)}, u32[]{:S(2)}) collective-permute-start(bf16[256,512]{0,1:T(8,128)(2,1)} %collective-permute-done.11), channel_id=1, source_target_pairs={{0,4},{2,254},{4,8},{6,2},{8,12},{10,6},{12,16},{14,10},{16,20},{1... | collective-permute-start | bytes 786440 | tf_op jit(solution)/shard_map/ppermute | solution.py:28
  68.5 25.2 %collective-permute-start.16 = (bf16[256,512]{0,1:T(8,128)(2,1)}, bf16[256,512]{0,1:T(8,128)(2,1)}, u32[]{:S(2)}, u32[]{:S(2)}) collective-permute-start(bf16[256,512]{0,1:T(8,128)(2,1)} %collective-permute-done.12), channel_id=1, source_target_pairs={{0,4},{2,254},{4,8},{6,2},{8,12},{10,6},{12,16},{14,10},{16,20},{1... | collective-permute-start | bytes 786440 | tf_op jit(solution)/shard_map/ppermute | solution.py:28
  102.3 7.3 %collective-permute-start.17 = (f32[512,512]{0,1:T(8,128)S(1)}, f32[512,512]{0,1:T(8,128)S(1)}, u32[]{:S(2)}, u32[]{:S(2)}) collective-permute-start(f32[512,512]{0,1:T(8,128)S(1)} %get-tuple-element.10), channel_id=1, source_target_pairs={{0,2},{2,0},{1,3},{3,1},{4,6},{6,4},{5,7},{7,5},{8,10},{10,8},{9,1... | collective-permute-start | bytes 3145736 | tf_op jit(solution)/shard_map/ppermute | solution.py:32
  107.2 60.7 %collective-permute-start.19 = (bf16[512,768]{1,0:T(8,128)(2,1)}, bf16[512,768]{1,0:T(8,128)(2,1)}, u32[]{:S(2)}, u32[]{:S(2)}) collective-permute-start(bf16[512,768]{1,0:T(8,128)(2,1)} %param.6), channel_id=1, source_target_pairs={{0,2},{2,0},{1,3},{3,1},{4,6},{6,4},{5,7},{7,5},{8,10},{10,8},{9,1... | collective-permute-start | bytes 2359304 | tf_op jit(solution)/shard_map/ppermute | solution.py:32
  167.2 3.3 %collective-permute-start.18 = (bf16[1024,512]{0,1:T(8,128)(2,1)S(1)}, bf16[1024,512]{0,1:T(8,128)(2,1)}, u32[]{:S(2)}, u32[]{:S(2)}) collective-permute-start(bf16[1024,512]{0,1:T(8,128)(2,1)S(1)} %pad_maximum_fusion), channel_id=1, source_target_pairs={{0,2},{2,0},{1,3},{3,1},{4,6},{6,4},{5,7},{7,5},{8,10},{10,8},{9,1... | collective-permute-start | bytes 3145736 | tf_op jit(solution)/shard_map/ppermute | solution.py:32
  174.9 31.0 %all-to-all-start = ((bf16[3,128,512]{2,0,1:T(4,128)(2,1)}), bf16[3,128,512]{2,0,1:T(4,128)(2,1)S(1)}, u32[]{:S(2)}, u32[]{:S(2)}) async-start(bf16[3,128,512]{2,0,1:T(4,128)(2,1)} %copy.82), calls=%async_computation | async-start | bytes 1048576 | tf_op jit(solution)/shard_map/all_to_all | solution.py:120

commit v2 on v1

v2 whole, which is shorter than its diff:
```python
import functools

import jax
import jax.numpy as jnp
from jax import lax
from jax.experimental import pallas as pl
from jax.experimental.pallas import tpu as pltpu
from jax.sharding import Mesh, PartitionSpec as P

EPS = 1e-06
SHIFTS = 8
PIECE = 256
AXES = ("x", "yl", "z", "c", "yh")
DP = ("x", "yl", "z", "c")
PLANE = ("x", "yl", "yh")
SIZES = (4, 2, 8, 2, 2)
BF16, F32 = jnp.bfloat16, jnp.float32
SCALARS = pl.BlockSpec(memory_space=pltpu.SMEM)
LIMIT = pltpu.CompilerParams(vmem_limit_bytes=20 << 20)


def row_sum(values):
    return jnp.sum(values, axis=-1, keepdims=True)


def unit_rows(values):
    factor = lax.rsqrt(row_sum(values * values) + EPS)
    return (values * factor, factor)


def back_rows(normal, factor, upstream):
    return factor * (upstream - normal * row_sum(normal * upstream))


def next_chip(block):
    chips = lax.axis_size(DP) // 2
    route = [(2 * i + c, 2 * ((i + (1, -1)[c]) % chips) + c) for i in range(chips) for c in (0, 1)]
    return lax.ppermute(block, DP, route)


def other_core(block):
    return lax.ppermute(block, "c", [(0, 1), (1, 0)])


def cost(flops, nbytes):
    return pl.CostEstimate(flops=flops, bytes_accessed=nbytes, transcendentals=0)


def units_kernel(core_ref, image_ref, feats_ref, proj_ref, stream_ref, still_ref, own_ref, cross_ref):
    image = image_ref[...].astype(F32)
    text = jnp.dot(feats_ref[...], proj_ref[...], preferred_element_type=F32)
    u = unit_rows(image)[0].astype(BF16)
    v = unit_rows(text)[0].astype(BF16)

    @pl.when(core_ref[0] == 0)
    def _():
        stream_ref[...], still_ref[...] = v, u
        own_ref[...], cross_ref[...] = image, text

    @pl.when(core_ref[0] != 0)
    def _():
        stream_ref[...], still_ref[...] = u, v
        own_ref[...], cross_ref[...] = text, image


def units(core, images, feats, proj, part):
    width = proj.shape[1]
    shape = lambda dtype: jax.ShapeDtypeStruct((PIECE, width), dtype)
    pick = lambda array: pl.BlockSpec((PIECE, array.shape[1]), lambda i: (part, 0))
    out = pl.BlockSpec((PIECE, width), lambda i: (0, 0))
    return pl.pallas_call(
        units_kernel,
        grid=(1,),
        out_shape=[shape(BF16), shape(BF16), shape(F32), shape(F32)],
        in_specs=[SCALARS, pick(images), pick(feats), pl.BlockSpec(proj.shape, lambda i: (0, 0))],
        out_specs=[out] * 4,
        compiler_params=LIMIT,
        cost_estimate=cost(2 * PIECE * proj.shape[0] * width, 2 << 20),
        name=f"units{part}",
    )(core, images, feats, proj)


def term(scalars, still, held, offset=None):
    scale, bias = scalars[0], scalars[1]
    logits = lax.dot_general(still, held, (((1,), (1,)), ((), ())), preferred_element_type=F32)
    logits = scale * logits + bias
    if offset is None:
        weighted = scale / (1.0 + jnp.exp(-logits))
    else:
        rows = lax.broadcasted_iota(jnp.int32, logits.shape, 0)
        cols = lax.broadcasted_iota(jnp.int32, logits.shape, 1)
        label = jnp.where(rows + offset == cols, 1.0, -1.0)
        weighted = -label * scale / (1.0 + jnp.exp(label * logits))
    return jnp.dot(weighted.astype(BF16), held, preferred_element_type=F32)


def first_kernel(per, scalars, still_ref, *refs):
    held, out_ref = refs[:-1], refs[-1]
    i = pl.program_id(0)

    @pl.when(i < per)
    def _():
        out_ref[...] = sum(
            term(scalars, still_ref[...], held[j][...], (i - j) * PIECE) for j in range(per)
        )

    @pl.when(i >= per)
    def _():
        still = still_ref[...]
        out_ref[...] = sum(term(scalars, still, held[j][...]) for j in range(per)) + sum(
            term(scalars, still, held[per + j][...], (i - per - j) * PIECE) for j in range(per)
        )


def hop_kernel(scalars, still_ref, sums_ref, *refs):
    held, out_ref = refs[:-1], refs[-1]
    still = still_ref[...]
    out_ref[...] = sums_ref[...] + sum(term(scalars, still, h[...]) for h in held)


def last_kernel(scalars, still_ref, raw_ref, sums_ref, *refs):
    held, out_ref = refs[:-1], refs[-1]
    still = still_ref[...]
    upstream = sums_ref[...] + sum(term(scalars, still, h[...]) for h in held)
    normal, factor = unit_rows(raw_ref[...])
    out_ref[...] = back_rows(normal, factor, upstream).astype(BF16)


def tiles(kernel, scalars, streamed, held, dtype, blocks, alias=None, name=None):
    width = held[0].shape[1]
    row = pl.BlockSpec((PIECE, width), lambda i: (i, 0))
    whole = pl.BlockSpec((PIECE, width), lambda i: (0, 0))
    rows = streamed[0].shape[0]
    return pl.pallas_call(
        kernel,
        grid=(blocks,),
        out_shape=jax.ShapeDtypeStruct((rows, width), dtype),
        in_specs=[SCALARS] + [row] * len(streamed) + [whole] * len(held),
        out_specs=row,
        input_output_aliases={} if alias is None else {alias: 0},
        compiler_params=LIMIT,
        cost_estimate=cost(4 * len(held) * blocks * PIECE * PIECE * width, 6 << 20),
        name=name,
    )(scalars, *streamed, *held)


def proj_kernel(core_ref, feats_ref, mine_ref, crossed_ref, out_ref, sum_ref):
    i = pl.program_id(0)
    grads = jnp.where(core_ref[0] == 0, crossed_ref[...], mine_ref[...])
    part = lax.dot_general(
        feats_ref[...], grads, (((0,), (0,)), ((), ())), preferred_element_type=F32
    )

    @pl.when(i == 0)
    def _():
        sum_ref[...] = part

    @pl.when(i > 0)
    def _():
        sum_ref[...] += part

    @pl.when(i == pl.num_programs(0) - 1)
    def _():
        out_ref[...] = sum_ref[...].astype(BF16)


def proj_part(core, feats, mine, crossed):
    depth, rows = feats.shape
    width = mine.shape[1]
    block = lambda n: pl.BlockSpec((PIECE, n), lambda i: (i, 0))
    return pl.pallas_call(
        proj_kernel,
        grid=(depth // PIECE,),
        out_shape=jax.ShapeDtypeStruct((rows, width), BF16),
        in_specs=[SCALARS, block(rows), block(width), block(width)],
        out_specs=pl.BlockSpec((rows, width), lambda i: (0, 0)),
        scratch_shapes=[pltpu.VMEM((rows, width), F32)],
        compiler_params=LIMIT,
        cost_estimate=cost(2 * depth * rows * width, 3 << 20),
        name="proj",
    )(core, feats, mine, crossed)


def on_device(images, text_feats, text_proj, logit_scale, logit_bias):
    core_id = lax.axis_index("c").astype(jnp.int32)
    core = core_id.reshape(1)
    first = core_id == 0
    rows = images.shape[0]
    per = rows // PIECE
    scalars = jnp.concatenate([logit_scale, logit_bias])

    stream, still, raw, cross = zip(
        *(units(core, images, text_feats, text_proj, i) for i in range(per))
    )
    held = list(stream)
    moving = [next_chip(b) for b in held]
    sibling = [other_core(b) for b in still]
    held += sibling
    moving += [next_chip(b) for b in sibling]
    still = jnp.concatenate(still + tuple(other_core(b) for b in stream))
    raw = jnp.concatenate(raw + tuple(other_core(b) for b in cross))
    feats_sib = other_core(text_feats)

    sums = tiles(
        functools.partial(first_kernel, per), scalars, [still], held, F32, 2 * per, name="hop0"
    )
    last = SHIFTS // 2
    for hop in range(1, last):
        held = moving
        moving = [next_chip(b) for b in held]
        sums = tiles(hop_kernel, scalars, [still, sums], held, F32, 2 * per, 2, name=f"hop{hop}")
    sums = tiles(hop_kernel, scalars, [still, sums], moving[:per], F32, per, 2, name="hop4own")
    grads = tiles(
        last_kernel, scalars, [still, raw, sums], moving[per:], BF16, 2 * per, name="hop4sib"
    )

    feats = jnp.concatenate(
        [jnp.where(first, feats_sib, text_feats), jnp.where(first, text_feats, feats_sib)]
    )
    wide = text_feats.shape[1]
    deep, plane = lax.axis_size("z"), lax.axis_size(PLANE)
    each = wide // (2 * deep * plane)
    at = lax.broadcasted_iota(jnp.int32, (wide, wide // 2), 1)
    j, z, p = at % each, (at // each) % deep, at // (each * deep)
    owner = (((p // 2) * deep + z) * 2 + core_id) * 2 + p % 2
    pick = (lax.broadcasted_iota(jnp.int32, (wide, wide // 2), 0) == owner * each + j).astype(BF16)
    feats = jnp.dot(feats, pick, preferred_element_type=F32).astype(BF16)

    crossed = other_core(grads)
    part = proj_part(core, feats, grads, crossed)
    image_grad = jnp.where(first, grads[:rows], crossed[rows:])
    part = part.reshape(plane, deep * each, -1)
    part = lax.all_to_all(part, PLANE, 0, 0, tiled=True)
    part = jnp.sum(part.astype(F32), axis=0).reshape(deep, each, -1)
    part = lax.all_to_all(part, "z", 0, 0, tiled=True)
    return (image_grad, jnp.sum(part, axis=0))


def solution(mesh):
    fine = Mesh(mesh.devices.reshape(SIZES), AXES)
    split = P(AXES, None)
    in_specs = (split, split, P(), P(), P())
    return jax.shard_map(
        on_device, mesh=fine, in_specs=in_specs, out_specs=(split, split), check_vma=False
    )
```

time: 211 us -> 107 us (0.51); the launches traced: 207 us -> 106 us
  matrix products: 115 us -> 1.04 us
  Pallas kernels: 0 us -> 28.4 us
  waiting for transfers between devices: 25.7 us -> 9.25 us
  blocking collectives: 0 us -> 14.7 us
  starting transfers between devices: 49.2 us -> 43.4 us
  other arithmetic: 8.43 us -> 3.06 us
  local copies, waits for them, and re-layouts: 6.23 us -> 4.02 us
    dot_general x38 -> x1, matrix products: 115 us -> 1.04 us  [on_device(): feats = jnp.dot(feats, pick, preferred_element_type=F32).astype(BF16)]
    pallas_call x0 -> x9, Pallas kernels: none -> 28.4 us  [the longest x6 25.7 us: tiles(): pl.pallas_call(kernel, grid=(blocks,), out_shape=jax.ShapeDtypeStruct((ro...]
    all_to_all x0 -> x1, blocking collectives: none -> 14.7 us  [on_device(): part = lax.all_to_all(part, PLANE, 0, 0, tiled=True)]
    all_to_all x1, waiting for transfers between devices: 17.6 us -> 6.07 us  [on_device(): part = lax.all_to_all(part, 'z', 0, 0, tiled=True)]
    ppermute x16, starting transfers between devices: 32.1 us -> 21 us  [next_chip(): return lax.ppermute(block, DP, route)]
    ppermute x4 -> x8, starting transfers between devices: 5.85 us -> 13.6 us  [other_core(): return lax.ppermute(block, 'c', [(0, 1), (1, 0)])]
    ppermute x16, waiting for transfers between devices: 5.96 us -> 3.16 us  [next_chip(): return lax.ppermute(block, DP, route)]
    slice x2 -> x0, local copies, waits for them, and re-layouts: 2.73 us -> none  [on_device(): cut = lambda b: [b[i * step:(i + 1) * step] for i in range(PIECES)]]
  transfers between devices with their start and end apart: 21 -> 25, of which waited for: 5 -> 3; matrix products, arithmetic and copies ran while one was open for 56% -> 3% of each run, Pallas kernels for 0% -> 25%
where the time goes in v2:
time: 107 us; the launch traced here: 106 us
  starting transfers between devices  43.4 us (41%)
  Pallas kernels  28.4 us (27%)
  blocking collectives  14.7 us (14%)
  waiting for transfers between devices  9.25 us (9%)
  local copies, waits for them, and re-layouts  4.02 us (4%)
  other arithmetic  3.06 us (3%)
  between operations  2.22 us (2%)
    pallas_call x6, Pallas kernels, tiles(): pl.pallas_call(kernel, grid=(blocks,), out_shape=jax.ShapeDtypeStruct((ro...  25.7 us
    ppermute x16, starting transfers between devices, next_chip(): return lax.ppermute(block, DP, route)  21 us
    all_to_all x1, blocking collectives, on_device(): part = lax.all_to_all(part, PLANE, 0, 0, tiled=True)  14.7 us
    ppermute x8, starting transfers between devices, other_core(): return lax.ppermute(block, 'c', [(0, 1), (1, 0)])  13.6 us
    all_to_all x1, starting transfers between devices, on_device(): part = lax.all_to_all(part, 'z', 0, 0, tiled=True)  8.86 us
    all_to_all x1, waiting for transfers between devices, on_device(): part = lax.all_to_all(part, 'z', 0, 0, tiled=True)  6.07 us
    unnamed x11, local copies, waits for them, and re-layouts  3.36 us
    ppermute x16, waiting for transfers between devices, next_chip(): return lax.ppermute(block, DP, route)  3.16 us
  transfers between devices with their start and end apart: 25, of which 3 were waited for; matrix products, arithmetic and copies ran while one was open for 3% of the time, Pallas kernels for 25%

profile of v2, /device:TPU:32, one launch (start us, length us, event | category | flops | bytes accessed | tf_op | source)
XLA Modules:
  0.0 106.0 jit_solution(15899193093218443843)
XLA Ops:
  0.6 1.1 %copy-done = bf16[512,768]{1,0:T(8,128)(2,1)S(1)} copy-done((bf16[512,768]{1,0:T(8,128)(2,1)S(1)}, bf16[512,768]{1,0:T(8,128)(2,1)}, u32[]{:S(2)}) %copy-start) | copy-done | bytes 786456
  1.8 1.1 %copy-done.2 = bf16[768,512]{1,0:T(8,128)(2,1)S(1)} copy-done((bf16[768,512]{1,0:T(8,128)(2,1)S(1)}, bf16[768,512]{1,0:T(8,128)(2,1)}, u32[]{:S(2)}) %copy-start.2) | copy-done | bytes 786456
  2.9 1.0 copy-done.3
  6.4 2.0 %collective-permute-start.6 = (bf16[256,512]{1,0:T(8,128)(2,1)S(1)}, bf16[256,512]{1,0:T(8,128)(2,1)S(1)}, u32[]{:S(2)}, u32[]{:S(2)}) collective-permute-start(bf16[256,512]{1,0:T(8,128)(2,1)S(1)} %get-tuple-element.12.refs_0_), channel_id=1, source_target_pairs={{0,4},{2,254},{4,8},{6,2},{8,12},{10,6},{12,16},{14,10},{16,20},{1... | collective-permute-start | bytes 786440 | tf_op jit(solution)/shard_map/ppermute | solution.py:38
  9.8 2.0 %collective-permute-start.7 = (bf16[256,512]{1,0:T(8,128)(2,1)S(1)}, bf16[256,512]{1,0:T(8,128)(2,1)S(1)}, u32[]{:S(2)}, u32[]{:S(2)}) collective-permute-start(bf16[256,512]{1,0:T(8,128)(2,1)S(1)} %get-tuple-element.13.refs_1_), channel_id=1, source_target_pairs={{0,4},{2,254},{4,8},{6,2},{8,12},{10,6},{12,16},{14,10},{16,20},{1... | collective-permute-start | bytes 786440 | tf_op jit(solution)/shard_map/ppermute | solution.py:38
  11.8 3.1 %collective-permute-start.8 = (bf16[256,512]{1,0:T(8,128)(2,1)S(1)}, bf16[256,512]{1,0:T(8,128)(2,1)S(1)}, u32[]{:S(2)}, u32[]{:S(2)}) collective-permute-start(bf16[256,512]{1,0:T(8,128)(2,1)S(1)} %collective-permute-done.4.refs_2_), channel_id=1, source_target_pairs={{0,4},{2,254},{4,8},{6,2},{8,12},{10,6},{12,16},{14,10},{16,20},{1... | collective-permute-start | bytes 786440 | tf_op jit(solution)/shard_map/ppermute | solution.py:38
  14.9 1.0 collective-permute-start.9
  16.0 2.6 %collective-permute-start.2 = (f32[256,512]{1,0:T(8,128)S(1)}, f32[256,512]{1,0:T(8,128)S(1)}, u32[]{:S(2)}, u32[]{:S(2)}) collective-permute-start(f32[256,512]{1,0:T(8,128)S(1)} %get-tuple-element.16), channel_id=1, source_target_pairs={{0,2},{2,0},{1,3},{3,1},{4,6},{6,4},{5,7},{7,5},{8,10},{10,8},{9,1... | collective-permute-start | bytes 1572872 | tf_op jit(solution)/shard_map/ppermute | solution.py:42
  18.6 1.1 %collective-permute-start.10 = (bf16[256,512]{1,0:T(8,128)(2,1)S(1)}, bf16[256,512]{1,0:T(8,128)(2,1)S(1)}, u32[]{:S(2)}, u32[]{:S(2)}) collective-permute-start(bf16[256,512]{1,0:T(8,128)(2,1)S(1)} %collective-permute-done.6.refs_0_), channel_id=1, source_target_pairs={{0,4},{2,254},{4,8},{6,2},{8,12},{10,6},{12,16},{14,10},{16,20},{1... | collective-permute-start | bytes 786440 | tf_op jit(solution)/shard_map/ppermute | solution.py:38
  19.7 1.5 %collective-permute-start.11 = (bf16[256,512]{1,0:T(8,128)(2,1)S(1)}, bf16[256,512]{1,0:T(8,128)(2,1)S(1)}, u32[]{:S(2)}, u32[]{:S(2)}) collective-permute-start(bf16[256,512]{1,0:T(8,128)(2,1)S(1)} %collective-permute-done.7.refs_1_), channel_id=1, source_target_pairs={{0,4},{2,254},{4,8},{6,2},{8,12},{10,6},{12,16},{14,10},{16,20},{1... | collective-permute-start | bytes 786440 | tf_op jit(solution)/shard_map/ppermute | solution.py:38
  21.3 2.6 %collective-permute-start.12 = (bf16[256,512]{1,0:T(8,128)(2,1)S(1)}, bf16[256,512]{1,0:T(8,128)(2,1)S(1)}, u32[]{:S(2)}, u32[]{:S(2)}) collective-permute-start(bf16[256,512]{1,0:T(8,128)(2,1)S(1)} %collective-permute-done.8.refs_2_), channel_id=1, source_target_pairs={{0,4},{2,254},{4,8},{6,2},{8,12},{10,6},{12,16},{14,10},{16,20},{1... | collective-permute-start | bytes 786440 | tf_op jit(solution)/shard_map/ppermute | solution.py:38
  24.4 4.1 %hop0.1.sums_ref = f32[1024,512]{1,0:T(8,128)S(1)} custom-call(f32[2]{0:T(128)S(1)} %pad_maximum_fusion.1.scalars, bf16[1024,512]{1,0:T(8,128)(2,1)S(1)} %constant_dynamic-update-slice_fusion.still_ref, bf16[256,512]{1,0:T(8,128)(2,1)S(1)} %get-tuple-element.12.refs_0_, bf16[256,512]{1,0:T(8,128)(2,1)S(1)} %get-tuple-element.13.refs_1_, ...), custom_call_target="tpu_custom_call" | custom-call | flops 2147483648 | bytes 6291456 | tf_op jit(solution)/shard_map/hop0/pallas_call | solution.py:134
  28.6 2.7 %collective-permute-start.14 = (bf16[256,512]{1,0:T(8,128)(2,1)S(1)}, bf16[256,512]{1,0:T(8,128)(2,1)S(1)}, u32[]{:S(2)}, u32[]{:S(2)}) collective-permute-start(bf16[256,512]{1,0:T(8,128)(2,1)S(1)} %collective-permute-done.10.refs_0_), channel_id=1, source_target_pairs={{0,4},{2,254},{4,8},{6,2},{8,12},{10,6},{12,16},{14,10},{16,20},{1... | collective-permute-start | bytes 786440 | tf_op jit(solution)/shard_map/ppermute | solution.py:38
  31.3 2.6 %collective-permute-start.15 = (bf16[256,512]{1,0:T(8,128)(2,1)S(1)}, bf16[256,512]{1,0:T(8,128)(2,1)S(1)}, u32[]{:S(2)}, u32[]{:S(2)}) collective-permute-start(bf16[256,512]{1,0:T(8,128)(2,1)S(1)} %collective-permute-done.11.refs_1_), channel_id=1, source_target_pairs={{0,4},{2,254},{4,8},{6,2},{8,12},{10,6},{12,16},{14,10},{16,20},{1... | collective-permute-start | bytes 786440 | tf_op jit(solution)/shard_map/ppermute | solution.py:38
  34.0 1.6 %collective-permute-done.13.refs_3_ = bf16[256,512]{1,0:T(8,128)(2,1)S(1)} collective-permute-done((bf16[256,512]{1,0:T(8,128)(2,1)S(1)}, bf16[256,512]{1,0:T(8,128)(2,1)S(1)}, u32[]{:S(2)}, u32[]{:S(2)}) %collective-permute-start.13) | collective-permute-done | bytes 262176 | tf_op jit(solution)/shard_map/ppermute | solution.py:38
  35.6 5.4 %hop1.1.sums_ref = f32[1024,512]{1,0:T(8,128)S(1)} custom-call(f32[2]{0:T(128)S(1)} %pad_maximum_fusion.1.scalars, bf16[1024,512]{1,0:T(8,128)(2,1)S(1)} %constant_dynamic-update-slice_fusion.still_ref, f32[1024,512]{1,0:T(8,128)S(1)} %hop0.1.sums_ref, bf16[256,512]{1,0:T(8,128)(2,1)S(1)} %collective-permute-done.6.refs_0_, ...), custom_call_target="tpu_custom_call", output_to_operand_aliasing={{}: (2, {})} | custom-call | flops 2147483648 | bytes 6291456 | tf_op jit(solution)/shard_map/hop1/pallas_call | solution.py:134
  41.1 7.3 %collective-permute-start.23 = (bf16[512,768]{1,0:T(8,128)(2,1)S(1)}, bf16[512,768]{1,0:T(8,128)(2,1)}, u32[]{:S(2)}, u32[]{:S(2)}) collective-permute-start(bf16[512,768]{1,0:T(8,128)(2,1)S(1)} %copy-done.1), channel_id=1, source_target_pairs={{0,2},{2,0},{1,3},{3,1},{4,6},{6,4},{5,7},{7,5},{8,10},{10,8},{9,1... | collective-permute-start | bytes 2359304 | tf_op jit(solution)/shard_map/ppermute | solution.py:42
  48.8 1.3 %collective-permute-start.20 = (bf16[256,512]{1,0:T(8,128)(2,1)S(1)}, bf16[256,512]{1,0:T(8,128)(2,1)S(1)}, u32[]{:S(2)}, u32[]{:S(2)}) collective-permute-start(bf16[256,512]{1,0:T(8,128)(2,1)S(1)} %collective-permute-done.16.refs_2_), channel_id=1, source_target_pairs={{0,4},{2,254},{4,8},{6,2},{8,12},{10,6},{12,16},{14,10},{16,20},{1... | collective-permute-start | bytes 786440 | tf_op jit(solution)/shard_map/ppermute | solution.py:38
  50.2 5.4 %hop2.1.sums_ref = f32[1024,512]{1,0:T(8,128)S(1)} custom-call(f32[2]{0:T(128)S(1)} %pad_maximum_fusion.1.scalars, bf16[1024,512]{1,0:T(8,128)(2,1)S(1)} %constant_dynamic-update-slice_fusion.still_ref, f32[1024,512]{1,0:T(8,128)S(1)} %hop1.1.sums_ref, bf16[256,512]{1,0:T(8,128)(2,1)S(1)} %collective-permute-done.10.refs_0_, ...), custom_call_target="tpu_custom_call", output_to_operand_aliasing={{}: (2, {})} | custom-call | flops 2147483648 | bytes 6291456 | tf_op jit(solution)/shard_map/hop2/pallas_call | solution.py:134
  55.7 5.4 %hop3.1.sums_ref = f32[1024,512]{1,0:T(8,128)S(1)} custom-call(f32[2]{0:T(128)S(1)} %pad_maximum_fusion.1.scalars, bf16[1024,512]{1,0:T(8,128)(2,1)S(1)} %constant_dynamic-update-slice_fusion.still_ref, f32[1024,512]{1,0:T(8,128)S(1)} %hop2.1.sums_ref, bf16[256,512]{1,0:T(8,128)(2,1)S(1)} %collective-permute-done.14.refs_0_, ...), custom_call_target="tpu_custom_call", output_to_operand_aliasing={{}: (2, {})} | custom-call | flops 2147483648 | bytes 6291456 | tf_op jit(solution)/shard_map/hop3/pallas_call | solution.py:134
  61.1 1.8 %hop4own.1.sums_ref = f32[1024,512]{1,0:T(8,128)S(1)} custom-call(f32[2]{0:T(128)S(1)} %pad_maximum_fusion.1.scalars, bf16[1024,512]{1,0:T(8,128)(2,1)S(1)} %constant_dynamic-update-slice_fusion.still_ref, f32[1024,512]{1,0:T(8,128)S(1)} %hop3.1.sums_ref, bf16[256,512]{1,0:T(8,128)(2,1)S(1)} %collective-permute-done.18.refs_0_, ...), custom_call_target="tpu_custom_call", output_to_operand_aliasing={{}: (2, {})} | custom-call | flops 536870912 | bytes 6291456 | tf_op jit(solution)/shard_map/hop4own/pallas_call | solution.py:134
  63.0 1.5 %collective-permute-done.21.refs_1_ = bf16[256,512]{1,0:T(8,128)(2,1)S(1)} collective-permute-done((bf16[256,512]{1,0:T(8,128)(2,1)S(1)}, bf16[256,512]{1,0:T(8,128)(2,1)S(1)}, u32[]{:S(2)}, u32[]{:S(2)}) %collective-permute-start.21) | collective-permute-done | bytes 262176 | tf_op jit(solution)/shard_map/ppermute | solution.py:38
  64.5 3.4 %hop4sib.1.mine_ref = bf16[1024,512]{1,0:T(8,128)(2,1)S(1)} custom-call(f32[2]{0:T(128)S(1)} %pad_maximum_fusion.1.scalars, bf16[1024,512]{1,0:T(8,128)(2,1)S(1)} %constant_dynamic-update-slice_fusion.still_ref, f32[1024,512]{1,0:T(8,128)S(1)} %pad_maximum_fusion.raw_ref, f32[1024,512]{1,0:T(8,128)S(1)} %hop4own.1.sums_ref, ...), custom_call_target="tpu_custom_call" | custom-call | flops 1073741824 | bytes 6291456 | tf_op jit(solution)/shard_map/hop4sib/pallas_call | solution.py:134
  68.0 2.4 %collective-permute-start.22 = (bf16[1024,512]{1,0:T(8,128)(2,1)S(1)}, bf16[1024,512]{1,0:T(8,128)(2,1)S(1)}, u32[]{:S(2)}, u32[]{:S(2)}) collective-permute-start(bf16[1024,512]{1,0:T(8,128)(2,1)S(1)} %hop4sib.1.mine_ref), channel_id=1, source_target_pairs={{0,2},{2,0},{1,3},{3,1},{4,6},{6,4},{5,7},{7,5},{8,10},{10,8},{9,1... | collective-permute-start | bytes 3145736 | tf_op jit(solution)/shard_map/ppermute | solution.py:42
  70.4 1.2 %broadcast_select_fusion.1 = (bf16[512,768]{1,0:T(8,128)(2,1)S(1)}, bf16[512,768]{1,0:T(8,128)(2,1)S(1)}) fusion(bf16[512,768]{1,0:T(8,128)(2,1)} %collective-permute-done.23, bf16[512,768]{1,0:T(8,128)(2,1)S(1)} %copy-done.1, pred[]{:T(512)S(6)} %eq.10), kind=kLoop, calls=%fused_computation.38 | loop fusion | flops 786432 | bytes 3145729 | tf_op jit(solution)/shard_map/jit(_where)/select_n | solution.py:218
  71.7 1.0 fusion.4.feats_ref
  72.7 1.5 %proj.1 = bf16[384,512]{1,0:T(8,128)(2,1)S(1)} custom-call(s32[1]{0:T(128)} %bitcast.core_ref, bf16[1024,384]{1,0:T(8,128)(2,1)S(1)} %fusion.4.feats_ref, bf16[1024,512]{1,0:T(8,128)(2,1)S(1)} %hop4sib.1.mine_ref, bf16[1024,512]{1,0:T(8,128)(2,1)S(1)} %collective-permute-done.22.crossed_ref), custom_call_target="tpu_custom_call" | custom-call | flops 402653184 | bytes 3145728 | tf_op jit(solution)/shard_map/proj/pallas_call | solution.py:171
  74.3 14.7 %all_to_all.10 = bf16[16,24,512]{2,1,0:T(8,128)(2,1)S(1)} all-to-all(bf16[16,24,512]{2,1,0:T(8,128)(2,1)S(1)} %bitcast.2), channel_id=1, replica_groups=mesh['x'=4,'yl'=2,'z'=8,'c'=2,'yh'=2] {'x','yl','yh'}, dimensions={0} | all-to-all | bytes 786432 | tf_op jit(solution)/shard_map/all_to_all | solution.py:233
  89.0 0.6 reshape.15
  89.6 8.9 %all-to-all-start.1 = ((f32[8,3,512]{2,1,0:T(4,128)}), f32[8,3,512]{2,1,0:T(4,128)S(1)}, u32[]{:S(2)}, u32[]{:S(2)}) async-start(f32[8,3,512]{2,1,0:T(4,128)} %reshape.15), calls=%async_computation.1 | async-start | bytes 131072 | tf_op jit(solution)/shard_map/all_to_all | solution.py:235
  98.5 0.8 slice_select_fusion
  99.4 6.1 %all-to-all-done.1 = f32[8,3,512]{2,1,0:T(4,128)S(1)} async-done(((f32[8,3,512]{2,1,0:T(4,128)}), f32[8,3,512]{2,1,0:T(4,128)S(1)}, u32[]{:S(2)}, u32[]{:S(2)}) %all-to-all-start.1) | async-done | bytes 49184 | tf_op jit(solution)/shard_map/all_to_all | solution.py:235
  (53 shorter events, 4.4 us)
Async XLA Ops:
  0.6 1.1 %copy-start = (bf16[512,768]{1,0:T(8,128)(2,1)S(1)}, bf16[512,768]{1,0:T(8,128)(2,1)}, u32[]{:S(2)}) copy-start(bf16[512,768]{1,0:T(8,128)(2,1)} %feats_ref.3) | copy-start | bytes 2359300
  1.8 1.1 %copy-start.2 = (bf16[768,512]{1,0:T(8,128)(2,1)S(1)}, bf16[768,512]{1,0:T(8,128)(2,1)}, u32[]{:S(2)}) copy-start(bf16[768,512]{1,0:T(8,128)(2,1)} %proj_ref.3) | copy-start | bytes 2359300
  2.9 1.0 copy-start.3
  4.5 1.9 %collective-permute-start = (bf16[256,512]{1,0:T(8,128)(2,1)S(1)}, bf16[256,512]{1,0:T(8,128)(2,1)S(1)}, u32[]{:S(2)}, u32[]{:S(2)}) collective-permute-start(bf16[256,512]{1,0:T(8,128)(2,1)S(1)} %get-tuple-element.12.refs_0_), channel_id=1, source_target_pairs={{0,2},{2,0},{1,3},{3,1},{4,6},{6,4},{5,7},{7,5},{8,10},{10,8},{9,1... | collective-permute-start | bytes 786440 | tf_op jit(solution)/shard_map/ppermute | solution.py:42
  5.2 4.6 %collective-permute-start.1 = (bf16[256,512]{1,0:T(8,128)(2,1)S(1)}, bf16[256,512]{1,0:T(8,128)(2,1)S(1)}, u32[]{:S(2)}, u32[]{:S(2)}) collective-permute-start(bf16[256,512]{1,0:T(8,128)(2,1)S(1)} %get-tuple-element.13.refs_1_), channel_id=1, source_target_pairs={{0,2},{2,0},{1,3},{3,1},{4,6},{6,4},{5,7},{7,5},{8,10},{10,8},{9,1... | collective-permute-start | bytes 786440 | tf_op jit(solution)/shard_map/ppermute | solution.py:42
  5.8 14.0 %collective-permute-start.3 = (f32[256,512]{1,0:T(8,128)S(1)}, f32[256,512]{1,0:T(8,128)S(1)}, u32[]{:S(2)}, u32[]{:S(2)}) collective-permute-start(f32[256,512]{1,0:T(8,128)S(1)} %get-tuple-element.17), channel_id=1, source_target_pairs={{0,2},{2,0},{1,3},{3,1},{4,6},{6,4},{5,7},{7,5},{8,10},{10,8},{9,1... | collective-permute-start | bytes 1572872 | tf_op jit(solution)/shard_map/ppermute | solution.py:42
  5.9 5.9 %collective-permute-start.4 = (bf16[256,512]{1,0:T(8,128)(2,1)S(1)}, bf16[256,512]{1,0:T(8,128)(2,1)S(1)}, u32[]{:S(2)}, u32[]{:S(2)}) collective-permute-start(bf16[256,512]{1,0:T(8,128)(2,1)S(1)} %get-tuple-element.10), channel_id=1, source_target_pairs={{0,2},{2,0},{1,3},{3,1},{4,6},{6,4},{5,7},{7,5},{8,10},{10,8},{9,1... | collective-permute-start | bytes 786440 | tf_op jit(solution)/shard_map/ppermute | solution.py:42
  6.3 8.6 %collective-permute-start.5 = (bf16[256,512]{1,0:T(8,128)(2,1)S(1)}, bf16[256,512]{1,0:T(8,128)(2,1)S(1)}, u32[]{:S(2)}, u32[]{:S(2)}) collective-permute-start(bf16[256,512]{1,0:T(8,128)(2,1)S(1)} %get-tuple-element.11), channel_id=1, source_target_pairs={{0,2},{2,0},{1,3},{3,1},{4,6},{6,4},{5,7},{7,5},{8,10},{10,8},{9,1... | collective-permute-start | bytes 786440 | tf_op jit(solution)/shard_map/ppermute | solution.py:42
  6.4 9.6 %collective-permute-start.6 = (bf16[256,512]{1,0:T(8,128)(2,1)S(1)}, bf16[256,512]{1,0:T(8,128)(2,1)S(1)}, u32[]{:S(2)}, u32[]{:S(2)}) collective-permute-start(bf16[256,512]{1,0:T(8,128)(2,1)S(1)} %get-tuple-element.12.refs_0_), channel_id=1, source_target_pairs={{0,4},{2,254},{4,8},{6,2},{8,12},{10,6},{12,16},{14,10},{16,20},{1... | collective-permute-start | bytes 786440 | tf_op jit(solution)/shard_map/ppermute | solution.py:38
  9.8 8.9 %collective-permute-start.7 = (bf16[256,512]{1,0:T(8,128)(2,1)S(1)}, bf16[256,512]{1,0:T(8,128)(2,1)S(1)}, u32[]{:S(2)}, u32[]{:S(2)}) collective-permute-start(bf16[256,512]{1,0:T(8,128)(2,1)S(1)} %get-tuple-element.13.refs_1_), channel_id=1, source_target_pairs={{0,4},{2,254},{4,8},{6,2},{8,12},{10,6},{12,16},{14,10},{16,20},{1... | collective-permute-start | bytes 786440 | tf_op jit(solution)/shard_map/ppermute | solution.py:38
  11.8 9.5 %collective-permute-start.8 = (bf16[256,512]{1,0:T(8,128)(2,1)S(1)}, bf16[256,512]{1,0:T(8,128)(2,1)S(1)}, u32[]{:S(2)}, u32[]{:S(2)}) collective-permute-start(bf16[256,512]{1,0:T(8,128)(2,1)S(1)} %collective-permute-done.4.refs_2_), channel_id=1, source_target_pairs={{0,4},{2,254},{4,8},{6,2},{8,12},{10,6},{12,16},{14,10},{16,20},{1... | collective-permute-start | bytes 786440 | tf_op jit(solution)/shard_map/ppermute | solution.py:38
  14.9 9.0 %collective-permute-start.9 = (bf16[256,512]{1,0:T(8,128)(2,1)S(1)}, bf16[256,512]{1,0:T(8,128)(2,1)S(1)}, u32[]{:S(2)}, u32[]{:S(2)}) collective-permute-start(bf16[256,512]{1,0:T(8,128)(2,1)S(1)} %collective-permute-done.5.refs_3_), channel_id=1, source_target_pairs={{0,4},{2,254},{4,8},{6,2},{8,12},{10,6},{12,16},{14,10},{16,20},{1... | collective-permute-start | bytes 786440 | tf_op jit(solution)/shard_map/ppermute | solution.py:38
  16.0 25.1 %collective-permute-start.2 = (f32[256,512]{1,0:T(8,128)S(1)}, f32[256,512]{1,0:T(8,128)S(1)}, u32[]{:S(2)}, u32[]{:S(2)}) collective-permute-start(f32[256,512]{1,0:T(8,128)S(1)} %get-tuple-element.16), channel_id=1, source_target_pairs={{0,2},{2,0},{1,3},{3,1},{4,6},{6,4},{5,7},{7,5},{8,10},{10,8},{9,1... | collective-permute-start | bytes 1572872 | tf_op jit(solution)/shard_map/ppermute | solution.py:42
  18.6 9.9 %collective-permute-start.10 = (bf16[256,512]{1,0:T(8,128)(2,1)S(1)}, bf16[256,512]{1,0:T(8,128)(2,1)S(1)}, u32[]{:S(2)}, u32[]{:S(2)}) collective-permute-start(bf16[256,512]{1,0:T(8,128)(2,1)S(1)} %collective-permute-done.6.refs_0_), channel_id=1, source_target_pairs={{0,4},{2,254},{4,8},{6,2},{8,12},{10,6},{12,16},{14,10},{16,20},{1... | collective-permute-start | bytes 786440 | tf_op jit(solution)/shard_map/ppermute | solution.py:38
  19.7 11.6 %collective-permute-start.11 = (bf16[256,512]{1,0:T(8,128)(2,1)S(1)}, bf16[256,512]{1,0:T(8,128)(2,1)S(1)}, u32[]{:S(2)}, u32[]{:S(2)}) collective-permute-start(bf16[256,512]{1,0:T(8,128)(2,1)S(1)} %collective-permute-done.7.refs_1_), channel_id=1, source_target_pairs={{0,4},{2,254},{4,8},{6,2},{8,12},{10,6},{12,16},{14,10},{16,20},{1... | collective-permute-start | bytes 786440 | tf_op jit(solution)/shard_map/ppermute | solution.py:38
  21.3 12.7 %collective-permute-start.12 = (bf16[256,512]{1,0:T(8,128)(2,1)S(1)}, bf16[256,512]{1,0:T(8,128)(2,1)S(1)}, u32[]{:S(2)}, u32[]{:S(2)}) collective-permute-start(bf16[256,512]{1,0:T(8,128)(2,1)S(1)} %collective-permute-done.8.refs_2_), channel_id=1, source_target_pairs={{0,4},{2,254},{4,8},{6,2},{8,12},{10,6},{12,16},{14,10},{16,20},{1... | collective-permute-start | bytes 786440 | tf_op jit(solution)/shard_map/ppermute | solution.py:38
  23.9 11.7 %collective-permute-start.13 = (bf16[256,512]{1,0:T(8,128)(2,1)S(1)}, bf16[256,512]{1,0:T(8,128)(2,1)S(1)}, u32[]{:S(2)}, u32[]{:S(2)}) collective-permute-start(bf16[256,512]{1,0:T(8,128)(2,1)S(1)} %collective-permute-done.9.refs_3_), channel_id=1, source_target_pairs={{0,4},{2,254},{4,8},{6,2},{8,12},{10,6},{12,16},{14,10},{16,20},{1... | collective-permute-start | bytes 786440 | tf_op jit(solution)/shard_map/ppermute | solution.py:38
  28.6 12.5 %copy-start.1 = (bf16[512,768]{1,0:T(8,128)(2,1)S(1)}, bf16[512,768]{1,0:T(8,128)(2,1)}, u32[]{:S(2)}) copy-start(bf16[512,768]{1,0:T(8,128)(2,1)} %feats_ref.3) | copy-start | bytes 2359300
  28.6 20.0 %collective-permute-start.14 = (bf16[256,512]{1,0:T(8,128)(2,1)S(1)}, bf16[256,512]{1,0:T(8,128)(2,1)S(1)}, u32[]{:S(2)}, u32[]{:S(2)}) collective-permute-start(bf16[256,512]{1,0:T(8,128)(2,1)S(1)} %collective-permute-done.10.refs_0_), channel_id=1, source_target_pairs={{0,4},{2,254},{4,8},{6,2},{8,12},{10,6},{12,16},{14,10},{16,20},{1... | collective-permute-start | bytes 786440 | tf_op jit(solution)/shard_map/ppermute | solution.py:38
  31.3 17.3 %collective-permute-start.15 = (bf16[256,512]{1,0:T(8,128)(2,1)S(1)}, bf16[256,512]{1,0:T(8,128)(2,1)S(1)}, u32[]{:S(2)}, u32[]{:S(2)}) collective-permute-start(bf16[256,512]{1,0:T(8,128)(2,1)S(1)} %collective-permute-done.11.refs_1_), channel_id=1, source_target_pairs={{0,4},{2,254},{4,8},{6,2},{8,12},{10,6},{12,16},{14,10},{16,20},{1... | collective-permute-start | bytes 786440 | tf_op jit(solution)/shard_map/ppermute | solution.py:38
  34.0 14.8 %collective-permute-start.16 = (bf16[256,512]{1,0:T(8,128)(2,1)S(1)}, bf16[256,512]{1,0:T(8,128)(2,1)S(1)}, u32[]{:S(2)}, u32[]{:S(2)}) collective-permute-start(bf16[256,512]{1,0:T(8,128)(2,1)S(1)} %collective-permute-done.12.refs_2_), channel_id=1, source_target_pairs={{0,4},{2,254},{4,8},{6,2},{8,12},{10,6},{12,16},{14,10},{16,20},{1... | collective-permute-start | bytes 786440 | tf_op jit(solution)/shard_map/ppermute | solution.py:38
  35.6 14.5 %collective-permute-start.17 = (bf16[256,512]{1,0:T(8,128)(2,1)S(1)}, bf16[256,512]{1,0:T(8,128)(2,1)S(1)}, u32[]{:S(2)}, u32[]{:S(2)}) collective-permute-start(bf16[256,512]{1,0:T(8,128)(2,1)S(1)} %collective-permute-done.13.refs_3_), channel_id=1, source_target_pairs={{0,4},{2,254},{4,8},{6,2},{8,12},{10,6},{12,16},{14,10},{16,20},{1... | collective-permute-start | bytes 786440 | tf_op jit(solution)/shard_map/ppermute | solution.py:38
  41.1 29.3 %collective-permute-start.23 = (bf16[512,768]{1,0:T(8,128)(2,1)S(1)}, bf16[512,768]{1,0:T(8,128)(2,1)}, u32[]{:S(2)}, u32[]{:S(2)}) collective-permute-start(bf16[512,768]{1,0:T(8,128)(2,1)S(1)} %copy-done.1), channel_id=1, source_target_pairs={{0,2},{2,0},{1,3},{3,1},{4,6},{6,4},{5,7},{7,5},{8,10},{10,8},{9,1... | collective-permute-start | bytes 2359304 | tf_op jit(solution)/shard_map/ppermute | solution.py:42
  48.6 12.5 %collective-permute-start.18 = (bf16[256,512]{1,0:T(8,128)(2,1)S(1)}, bf16[256,512]{1,0:T(8,128)(2,1)S(1)}, u32[]{:S(2)}, u32[]{:S(2)}) collective-permute-start(bf16[256,512]{1,0:T(8,128)(2,1)S(1)} %collective-permute-done.14.refs_0_), channel_id=1, source_target_pairs={{0,4},{2,254},{4,8},{6,2},{8,12},{10,6},{12,16},{14,10},{16,20},{1... | collective-permute-start | bytes 786440 | tf_op jit(solution)/shard_map/ppermute | solution.py:38
  48.7 12.4 %collective-permute-start.19 = (bf16[256,512]{1,0:T(8,128)(2,1)S(1)}, bf16[256,512]{1,0:T(8,128)(2,1)S(1)}, u32[]{:S(2)}, u32[]{:S(2)}) collective-permute-start(bf16[256,512]{1,0:T(8,128)(2,1)S(1)} %collective-permute-done.15.refs_1_), channel_id=1, source_target_pairs={{0,4},{2,254},{4,8},{6,2},{8,12},{10,6},{12,16},{14,10},{16,20},{1... | collective-permute-start | bytes 786440 | tf_op jit(solution)/shard_map/ppermute | solution.py:38
  48.8 14.2 %collective-permute-start.20 = (bf16[256,512]{1,0:T(8,128)(2,1)S(1)}, bf16[256,512]{1,0:T(8,128)(2,1)S(1)}, u32[]{:S(2)}, u32[]{:S(2)}) collective-permute-start(bf16[256,512]{1,0:T(8,128)(2,1)S(1)} %collective-permute-done.16.refs_2_), channel_id=1, source_target_pairs={{0,4},{2,254},{4,8},{6,2},{8,12},{10,6},{12,16},{14,10},{16,20},{1... | collective-permute-start | bytes 786440 | tf_op jit(solution)/shard_map/ppermute | solution.py:38
  50.1 14.4 %collective-permute-start.21 = (bf16[256,512]{1,0:T(8,128)(2,1)S(1)}, bf16[256,512]{1,0:T(8,128)(2,1)S(1)}, u32[]{:S(2)}, u32[]{:S(2)}) collective-permute-start(bf16[256,512]{1,0:T(8,128)(2,1)S(1)} %collective-permute-done.17.refs_3_), channel_id=1, source_target_pairs={{0,4},{2,254},{4,8},{6,2},{8,12},{10,6},{12,16},{14,10},{16,20},{1... | collective-permute-start | bytes 786440 | tf_op jit(solution)/shard_map/ppermute | solution.py:38
  68.0 4.7 %collective-permute-start.22 = (bf16[1024,512]{1,0:T(8,128)(2,1)S(1)}, bf16[1024,512]{1,0:T(8,128)(2,1)S(1)}, u32[]{:S(2)}, u32[]{:S(2)}) collective-permute-start(bf16[1024,512]{1,0:T(8,128)(2,1)S(1)} %hop4sib.1.mine_ref), channel_id=1, source_target_pairs={{0,2},{2,0},{1,3},{3,1},{4,6},{6,4},{5,7},{7,5},{8,10},{10,8},{9,1... | collective-permute-start | bytes 3145736 | tf_op jit(solution)/shard_map/ppermute | solution.py:42
  89.6 15.8 %all-to-all-start.1 = ((f32[8,3,512]{2,1,0:T(4,128)}), f32[8,3,512]{2,1,0:T(4,128)S(1)}, u32[]{:S(2)}, u32[]{:S(2)}) async-start(f32[8,3,512]{2,1,0:T(4,128)} %reshape.15), calls=%async_computation.1 | async-start | bytes 131072 | tf_op jit(solution)/shard_map/all_to_all | solution.py:235
